TPU v7x, 32 devices: a whole 2x2x4 slice. The times are simulated.
32 devices in a mesh: rep: 8 (over y, x, core), shard: 4 (over z).
Axes of the slice: x: 2, y: 2, z: 4, core: 2. Of those that a mesh axis runs over, the one named last changes fastest.
Arguments:
- teacher_states: bfloat16 [3072, 5120], P('rep'), may hold values from -16 to 16
- student_states: bfloat16 [3072, 3584], P('rep'), may hold values from -16 to 16
- teacher_gain: float32 [5120], replicated, may hold values from 0.25 to 1.75
- student_gain: float32 [3584], replicated, may hold values from 0.25 to 1.75
- teacher_query: bfloat16 [5120, 3072], P('rep', 'shard'), may hold values from -1 to 1
- teacher_key: bfloat16 [5120, 1024], P('rep', 'shard'), may hold values from -1 to 1
- teacher_value: bfloat16 [5120, 1024], P('rep', 'shard'), may hold values from -0.078125 to 0.078125
- teacher_output: bfloat16 [5120, 3072], P('rep', 'shard'), may hold values from -0.109375 to 0.109375
- student_query: bfloat16 [3584, 2048], P('rep', 'shard'), may hold values from -1 to 1
- student_key: bfloat16 [3584, 512], P('rep'), may hold values from -1 to 1
- student_value: bfloat16 [3584, 512], P('rep'), may hold values from -0.09375 to 0.09375
- student_output: bfloat16 [3584, 2048], P('rep', 'shard'), may hold values from -0.125 to 0.125
- projection: bfloat16 [3584, 5120], P('rep', 'shard'), may hold values from -0.09375 to 0.09375
Outputs:
- query_grad: float32 [3584, 2048], P('rep', 'shard')
- output_grad: float32 [3584, 2048], P('rep', 'shard')
All inputs are finite; a program needn't handle non-finite values.
Results may differ from a plain program's by a relative error of at most 0.023.
Values may be sent and summed in bfloat16 or wider, within the bound.
A program may use at most 128 MiB of HBM per device.

v0:
```python
from functools import partial
import math

import jax
import jax.numpy as jnp
from jax import lax
from jax.experimental import pallas as pl
from jax.experimental.pallas import tpu as pltpu
from jax.sharding import PartitionSpec as P

HQ_S = 16
KV_S = 4
HD = 128

theta_base = 1000000.0
norm_epsilon = 1e-06

F32 = jnp.float32
BF16 = jnp.bfloat16
VMEM_BYTES = 66 * 1000 * 1000
LAG = 2


def tables(length):
    halfway = HD // 2
    inverse = theta_base ** (-(jnp.arange(halfway, dtype=F32) * 2.0 / HD))
    angles = jnp.arange(length, dtype=F32)[:, None] * inverse[None, :]
    cosine = jnp.cos(angles)
    sine = jnp.sin(angles)
    return (
        jnp.concatenate([cosine, cosine], axis=1),
        jnp.concatenate([-sine, sine], axis=1),
    )


def rotate(values, cosine, sine):
    length = values.shape[0]
    split = values.reshape(length, -1, HD)
    swapped = jnp.roll(split, HD // 2, axis=-1)
    turned = split * cosine[:, None, :] + swapped * sine[:, None, :]
    return turned.reshape(length, -1)


def attend(query_rot, keys, values, head_dim):
    length = query_rot.shape[0]
    kv_heads = keys.shape[1] // head_dim
    group_size = query_rot.shape[1] // head_dim // kv_heads
    queries = query_rot.astype(BF16).reshape(length, kv_heads, group_size, head_dim)
    key_heads = keys.reshape(length, kv_heads, head_dim)
    value_heads = values.reshape(length, kv_heads, head_dim)
    scores = jnp.einsum(
        "qkgd,skd->kgqs", queries, key_heads, preferred_element_type=F32
    ) * head_dim ** (-0.5)
    rows_index = jnp.arange(length)[:, None]
    column_index = jnp.arange(length)[None, :]
    scores = jnp.where(rows_index >= column_index, scores, -1e30)
    highest = jnp.max(scores, axis=-1, keepdims=True)
    weights = jnp.exp(scores - highest)
    probs = (weights / jnp.sum(weights, axis=-1, keepdims=True)).astype(BF16)
    mixed = jnp.einsum("kgqs,skd->qkgd", probs, value_heads, preferred_element_type=F32)
    return mixed.reshape(length, -1)


def halving_scatter(term, axis):
    count = lax.axis_size(axis)
    bits = count.bit_length() - 1
    here = lax.axis_index(axis)
    rows = term.shape[0] // count
    width = term.shape[1] // 2
    outs = []
    for half in range(2):
        part = term[:, half * width : (half + 1) * width].reshape((2,) * bits + (rows, width))
        left = list(range(bits - 1, -1, -1))
        order = [0] + (list(range(1, bits)) if half == 0 else list(range(bits - 1, 0, -1)))
        for bit in order:
            place = left.index(bit)
            left.remove(bit)
            mine = lax.rem(lax.div(here, 2**bit), 2)
            sent = lax.dynamic_index_in_dim(part, 1 - mine, place, keepdims=False)
            kept = lax.dynamic_index_in_dim(part, mine, place, keepdims=False)
            came = lax.ppermute(
                sent.astype(BF16), axis, [(i, i ^ (1 << bit)) for i in range(count)]
            )
            part = kept.astype(F32) + came.astype(F32)
        outs.append(part)
    return jnp.concatenate(outs, axis=1)


def tile_of(width):
    return 256 if width % 256 == 0 else 128


def dot_nt(left, right):
    return lax.dot_general(left, right, (((1,), (1,)), ((), ())), preferred_element_type=F32)


class Place:
    def __init__(self, reps, shards):
        self.reps = reps
        self.shards = shards
        self.chips = reps // 2
        self.r = lax.axis_index("rep")
        self.z = lax.axis_index("shard")
        chip = lax.div(self.r, 2)
        self.core = lax.rem(self.r, 2)
        row = lax.div(chip, 2)
        self.pos = 2 * row + lax.rem(lax.rem(chip, 2) + row, 2)
        self.partner = 2 * chip + 1 - self.core
        self.right = self.rep_at(1, self.core)
        self.left = self.rep_at(-1, self.core)

    def rep_at(self, step, core):
        place = lax.rem(self.pos + step + self.chips, self.chips)
        row = lax.div(place, 2)
        chip = 2 * row + lax.rem(lax.rem(place, 2) + row, 2)
        return 2 * chip + core

    def barrier(self, ring, line):
        sem = pltpu.get_barrier_semaphore()
        if ring:
            for target in (self.partner, self.left, self.right):
                pl.semaphore_signal(sem, inc=1, device_id={"rep": target})
        if line:

            @pl.when(self.z > 0)
            def _():
                pl.semaphore_signal(sem, inc=1, device_id={"shard": self.z - 1})

            @pl.when(self.z < self.shards - 1)
            def _():
                pl.semaphore_signal(sem, inc=1, device_id={"shard": self.z + 1})

        peers = 3 if ring else 0
        if line:
            peers += jnp.minimum(self.z, 1) + jnp.minimum(self.shards - 1 - self.z, 1)
        pl.semaphore_wait(sem, peers)


class Gather:
    def __init__(self, place, source, full, index, send_sem, recv_sem, local_sem):
        self.place = place
        self.source = source
        self.full = full
        self.index = index
        self.send_sem = send_sem
        self.recv_sem = recv_sem
        self.local_sem = local_sem
        self.rows = source.shape[0]
        self.half = place.chips // 2

    def slab(self, owner, part):
        if part is None:
            return self.full.at[pl.ds(pl.multiple_of(owner * self.rows, self.rows), self.rows)]
        rows = self.rows // 2
        return self.full.at[pl.ds(pl.multiple_of((2 * owner + part) * rows, rows), rows)]

    def copy(self, message, target, owner, part, source=None):
        slab = self.slab(owner, part)
        return pltpu.make_async_remote_copy(
            src_ref=slab if source is None else source,
            dst_ref=slab,
            send_sem=self.send_sem.at[self.index, message],
            recv_sem=self.recv_sem.at[self.index, message],
            device_id={"rep": target},
        )

    def part_of(self, step, way):
        return None if step < self.half else way

    def local(self):
        return pltpu.make_async_copy(
            self.source, self.slab(self.place.r, None), self.local_sem.at[self.index]
        )

    def start(self):
        p = self.place
        h = self.half
        self.copy(0, p.right, p.r, self.part_of(1, 0), self.source).start()
        self.copy(h, p.left, p.r, self.part_of(1, 1), self.source).start()
        self.copy(2 * h, p.partner, p.r, None, self.source).start()
        self.local().start()

    def relay(self, step):
        p = self.place
        h = self.half
        for way, sign, target in ((0, -1, p.right), (1, 1, p.left)):
            owner = p.rep_at(sign * step, p.core)
            base = way * h
            self.copy(base + step - 1, target, owner, self.part_of(step, way)).wait_recv()
            if step < h:
                self.copy(base + step, target, owner, self.part_of(step + 1, way)).start()
            self.copy(2 * h + base + step, p.partner, owner, self.part_of(step, way)).start()

    def finish(self):
        p = self.place
        h = self.half
        self.local().wait()
        self.copy(2 * h, p.partner, p.partner, None).wait_recv()
        for step in range(1, h + 1):
            for way, sign in ((0, -1), (1, 1)):
                owner = p.rep_at(sign * step, 1 - p.core)
                self.copy(
                    2 * h + way * h + step, p.partner, owner, self.part_of(step, way)
                ).wait_recv()

    def drain(self):
        p = self.place
        h = self.half
        for way, sign, target in ((0, -1, p.right), (1, 1, p.left)):
            for step in range(1, h + 1):
                owner = p.rep_at(sign * (step - 1), p.core)
                self.copy(way * h + step - 1, target, owner, self.part_of(step, way)).wait_send()
                owner = p.rep_at(sign * step, p.core)
                self.copy(
                    2 * h + way * h + step, p.partner, owner, self.part_of(step, way)
                ).wait_send()
        self.copy(2 * h, p.partner, p.r, None).wait_send()


def run_hooks(hooks, wave, last):
    for at, action in hooks:
        if at < last:
            pl.when(wave == at)(action)


def late_hooks(hooks, last):
    for at, action in hooks:
        if at >= last:
            action()


def line_sum(place, count, produce, consume, own, rightward, leftward, send_sem, recv_sem, hooks):
    z = place.z
    ends = place.shards - 1
    waves = count + LAG * ends

    def copy(way, j):
        buffer = (rightward, leftward)[way]
        return pltpu.make_async_remote_copy(
            src_ref=buffer.at[j],
            dst_ref=buffer.at[j],
            send_sem=send_sem.at[way, j],
            recv_sem=recv_sem.at[way, j],
            device_id={"shard": (z + 1, z - 1)[way]},
        )

    def has_before(way):
        return (z > 0, z < ends)[way]

    def has_after(way):
        return (z < ends, z > 0)[way]

    def valid(j):
        return (j >= 0) & (j < count)

    def wave_body(w, carry):
        at = (w - LAG * z, w - LAG * (ends - z))
        first = jnp.maximum(at[0], at[1])
        final = jnp.minimum(at[0], at[1])

        @pl.when(valid(first))
        def _():
            own[first] = produce(first).astype(BF16)

        for way in range(2):
            j = at[way]
            buffer = (rightward, leftward)[way]

            @pl.when(valid(j))
            def _():
                @pl.when(has_before(way))
                def _():
                    copy(way, j).wait_recv()
                    buffer[j] = (own[j].astype(F32) + buffer[j].astype(F32)).astype(BF16)

                @pl.when(jnp.logical_not(has_before(way)))
                def _():
                    buffer[j] = own[j]

                @pl.when(has_after(way))
                def _():
                    copy(way, j).start()

        @pl.when(valid(final))
        def _():
            total = rightward[final].astype(F32) + leftward[final].astype(F32)
            consume(final, total - own[final].astype(F32))

        run_hooks(hooks, w, waves)
        return carry

    lax.fori_loop(0, waves, wave_body, 0)
    late_hooks(hooks, waves)

    def drain(j, carry):
        for way in range(2):

            @pl.when(has_after(way))
            def _():
                copy(way, j).wait_send()

        return carry

    return lambda: lax.fori_loop(0, count, drain, 0)


def line_scatter(place, per_block, produce, own, rightward, leftward, send_sem, recv_sem, hooks):
    z = place.z
    ends = place.shards - 1
    waves = ends * per_block + LAG * ends

    def copy(way, q):
        buffer = (rightward, leftward)[way]
        return pltpu.make_async_remote_copy(
            src_ref=buffer.at[q],
            dst_ref=buffer.at[q],
            send_sem=send_sem.at[way, q],
            recv_sem=recv_sem.at[way, q],
            device_id={"shard": (z + 1, z - 1)[way]},
        )

    def first_own(t, carry):
        own[t] = produce(z * per_block + t).astype(BF16).astype(F32)
        return carry

    lax.fori_loop(0, per_block, first_own, 0)

    def wave_body(w, carry):
        for way in range(2):
            line = (z, ends - z)[way]
            q = w - LAG * line
            past = (ends - line) * per_block
            buffer = (rightward, leftward)[way]
            before = line > 0

            @pl.when((q >= 0) & (q < past))
            def _():
                block = lax.div(q, per_block)
                chunk = lax.rem(q, per_block)
                target = (ends - block, block)[way]
                term = produce(target * per_block + chunk).astype(BF16)

                @pl.when(before)
                def _():
                    copy(way, q).wait_recv()
                    buffer[q] = (term.astype(F32) + buffer[q].astype(F32)).astype(BF16)

                @pl.when(jnp.logical_not(before))
                def _():
                    buffer[q] = term

                copy(way, q).start()

            @pl.when(before & (q >= past) & (q < past + per_block))
            def _():
                copy(way, q).wait_recv()
                own[q - past] += buffer[q].astype(F32)

        run_hooks(hooks, w, waves)
        return carry

    lax.fori_loop(0, waves, wave_body, 0)
    late_hooks(hooks, waves)

    def finish():
        for way in range(2):
            line = (z, ends - z)[way]

            def drain(q, carry):
                copy(way, q).wait_send()
                return carry

            lax.fori_loop(0, (ends - line) * per_block, drain, 0)

    return finish


def normalise(states, gain, block=16):
    length, width = states.shape

    def body(i, carry):
        at = pl.ds(pl.multiple_of(i * block, block), block)
        rows = states[at, :].astype(F32)
        meansq = jnp.sum(rows * rows, axis=-1, keepdims=True) * (1.0 / width)
        states[at, :] = (rows * lax.rsqrt(meansq + norm_epsilon) * gain[...]).astype(BF16)
        return carry

    lax.fori_loop(0, length // block, body, 0)


def turned(values, cosine, sine):
    return values * cosine + pltpu.roll(values, HD // 2, 1) * sine


def project(normed, weight, out, cosine, sine, first, count, tile):
    def body(t, carry):
        at = pl.ds(pl.multiple_of(t * tile, tile), tile)
        value = jnp.dot(normed[...], weight[:, at], preferred_element_type=F32)
        if cosine is None:
            out[:, at] = value.astype(BF16)
        else:
            for head in range(tile // HD):
                part = turned(value[:, head * HD : (head + 1) * HD], cosine[...], sine[...])
                spot = pl.ds(pl.multiple_of(t * tile + head * HD, HD), HD)
                out[:, spot] = part.astype(BF16)
        return carry

    lax.fori_loop(first, first + count, body, 0)


def soft(scores):
    highest = jnp.max(scores, axis=-1, keepdims=True)
    weights = jnp.exp(scores - highest)
    return weights / jnp.sum(weights, axis=-1, keepdims=True)


def masked_scores(query, keys):
    scores = dot_nt(query, keys) * HD ** (-0.5)
    row = lax.broadcasted_iota(jnp.int32, scores.shape, 0)
    column = lax.broadcasted_iota(jnp.int32, scores.shape, 1)
    return jnp.where(row >= column, scores, -1e30)


def attention(queries, keys, values, mixed, first, count, group):
    def body(h, carry):
        at = pl.ds(pl.multiple_of(h * HD, HD), HD)
        kv = pl.ds(pl.multiple_of(lax.div(h, group) * HD, HD), HD)
        probs = soft(masked_scores(queries[:, at], keys[:, kv])).astype(BF16)
        mixed[:, at] = jnp.dot(probs, values[:, kv], preferred_element_type=F32).astype(BF16)
        return carry

    lax.fori_loop(first, first + count, body, 0)


def forward_kernel(
    sizes,
    states_s,
    states_t,
    gain_s,
    gain_t,
    cosine,
    sine,
    w_sq,
    w_sk,
    w_sv,
    w_so,
    w_tq,
    w_tk,
    w_tv,
    w_to,
    w_pj,
    map_full,
    output_full,
    hidden_out,
    attn_out,
    normed_out,
    query_s,
    key_s,
    value_s,
    mixed_s,
    sq,
    sk,
    sv,
    so,
    tq,
    tk,
    tv,
    to,
    normed_s,
    normed_t,
    hidden,
    own_s,
    right_s,
    left_s,
    query_t,
    key_t,
    value_t,
    mixed_t,
    attn_t,
    right_t,
    left_t,
    gather_send,
    gather_recv,
    gather_local,
    sum_send,
    sum_recv,
    scatter_send,
    scatter_recv,
    copies,
):
    reps, shards, kv_start_of = sizes
    place = Place(reps, shards)
    kv_width = sk.shape[1]
    kv_at = pl.ds(pl.multiple_of(kv_start_of(place.z), HD), kv_width)
    sources = (w_sq, w_sk.at[:, kv_at], w_sv.at[:, kv_at], w_so, w_tq, w_tk, w_tv, w_to, w_pj)
    fulls = (sq, sk, sv, so, tq, tk, tv, to, map_full)
    weights = [
        Gather(place, source, full, i, gather_send, gather_recv, gather_local)
        for i, (source, full) in enumerate(zip(sources, fulls))
    ]
    half = place.chips // 2
    groups = {"P0": weights[0:3], "P1": weights[3:4], "P2a": weights[5:7], "P2b": weights[4:5],
              "P3": weights[7:8], "P4": weights[8:9]}

    def start(name):
        for weight in groups[name]:
            weight.start()

    def relay(name, step):
        for weight in groups[name]:
            weight.relay(step)

    def finish(name):
        for step in range(2, half + 1):
            relay(name, step)
        for weight in groups[name]:
            weight.finish()

    in_s = pltpu.make_async_copy(states_s, normed_s, copies.at[0])
    in_h = pltpu.make_async_copy(states_s, hidden, copies.at[1])
    in_t = pltpu.make_async_copy(states_t, normed_t, copies.at[2])
    in_s.start()
    place.barrier(True, True)
    start("P0")
    in_h.start()
    in_t.start()
    in_s.wait()
    normalise(normed_s, gain_s)
    relay("P0", 1)
    start("P1")
    in_t.wait()
    normalise(normed_t, gain_t)
    finish("P0")
    tile = tile_of(sq.shape[1])
    kv_tile = tile_of(kv_width)
    project(normed_s, sk, key_s, cosine, sine, 0, kv_width // kv_tile, kv_tile)
    project(normed_s, sv, value_s, None, None, 0, kv_width // kv_tile, kv_tile)
    project(normed_s, sq, query_s, cosine, sine, 0, sq.shape[1] // tile, tile)
    out_n = pltpu.make_async_copy(normed_s, normed_out, copies.at[3])
    out_n.start()
    relay("P1", 1)
    start("P2a")
    start("P2b")
    heads = sq.shape[1] // HD
    attention(query_s, key_s, value_s, mixed_s, 0, heads, heads // (kv_width // HD))
    finish("P1")
    out_o = pltpu.make_async_copy(so, output_full, copies.at[4])
    out_o.start()
    in_h.wait()

    width = own_s.shape[2]

    def produce_s(j):
        rows = pl.ds(pl.multiple_of(j * width, width), width)
        return dot_nt(mixed_s[...], so[rows, :])

    def consume_s(j, total):
        at = pl.ds(pl.multiple_of(j * width, width), width)
        hidden[:, at] = (hidden[:, at].astype(F32) + total).astype(BF16)

    t_tile = tile_of(tq.shape[1])
    t_kv = tile_of(tk.shape[1])
    t_heads = tq.shape[1] // HD
    t_group = t_heads // (tk.shape[1] // HD)
    hooks = [
        (2, lambda: relay("P2a", 1)),
        (7, lambda: relay("P2b", 1)),
        (7, lambda: start("P3")),
        (9, lambda: finish("P2a")),
        (11, lambda: finish("P2b")),
    ]
    wave = 11
    for t in range(tk.shape[1] // t_kv):
        hooks.append((wave, partial(project, normed_t, tk, key_t, cosine, sine, t, 1, t_kv)))
        hooks.append((wave, partial(project, normed_t, tv, value_t, None, None, t, 1, t_kv)))
        wave += 1
    for t in range(tq.shape[1] // t_tile):
        hooks.append((wave, partial(project, normed_t, tq, query_t, cosine, sine, t, 1, t_tile)))
        wave += 1
    hooks.append((wave, lambda: relay("P3", 1)))
    hooks.append((wave, lambda: start("P4")))
    for h in range(t_heads):
        hooks.append((wave, partial(attention, query_t, key_t, value_t, mixed_t, h, 1, t_group)))
        wave += h % 2
    drain_s = line_sum(
        place, own_s.shape[0], produce_s, consume_s, own_s, right_s, left_s, sum_send, sum_recv, hooks
    )
    out_h = pltpu.make_async_copy(hidden, hidden_out, copies.at[5])
    out_h.start()
    finish("P3")

    width_t = attn_t.shape[2]

    def produce_t(j):
        rows = pl.ds(pl.multiple_of(j * width_t, width_t), width_t)
        return dot_nt(mixed_t[...], to[rows, :])

    drain_t = line_scatter(
        place, attn_t.shape[0], produce_t, attn_t, right_t, left_t, scatter_send, scatter_recv,
        [(3, lambda: relay("P4", 1)), (9, lambda: finish("P4"))],
    )
    out_a = pltpu.make_async_copy(attn_t, attn_out, copies.at[6])
    out_a.start()
    drain_s()
    drain_t()
    for weight in weights:
        weight.drain()
    for copy in (out_n, out_o, out_h, out_a):
        copy.wait()


def gradient_kernel(
    sizes, grad_pred, column_map, hidden_out, map_all, own, right, left, sum_send, sum_recv, copies
):
    reps, shards = sizes
    place = Place(reps, shards)
    inward = pltpu.make_async_copy(column_map, map_all, copies.at[0])
    inward.start()
    place.barrier(False, True)
    inward.wait()
    width = own.shape[2]

    def produce(j):
        rows = pl.ds(pl.multiple_of(j * width, width), width)
        return dot_nt(grad_pred[...], map_all[rows, :])

    def consume(j, total):
        at = pl.ds(pl.multiple_of(j * width, width), width)
        hidden_out[:, at] = total.astype(BF16)

    line_sum(place, own.shape[0], produce, consume, own, right, left, sum_send, sum_recv, [])()


def local(
    reps,
    shards,
    teacher_states,
    student_states,
    teacher_gain,
    student_gain,
    teacher_query,
    teacher_key,
    teacher_value,
    teacher_output,
    student_query,
    student_key,
    student_value,
    student_output,
    projection,
):
    shard_index = lax.axis_index("shard")
    length, d_t = teacher_states.shape
    d_s = student_states.shape[1]
    local_heads = student_query.shape[1] // HD
    group_size = HQ_S // KV_S
    kv_width = max(local_heads // group_size, 1) * HD

    def kv_start_of(z):
        return lax.div(z * local_heads, group_size) * HD

    cosine, sine = tables(length)
    heads_s = student_query.shape[1]
    heads_t = teacher_query.shape[1]
    kv_t = teacher_key.shape[1]
    block_width = projection.shape[1]
    wide_s = tile_of(d_s)
    wide_t = tile_of(block_width)
    count_s = d_s // wide_s
    per_block = block_width // wide_t
    most = (shards - 1) * per_block
    messages = 4 * (reps // 4) + 1
    any_spec = pl.BlockSpec(memory_space=pl.ANY)
    vmem_spec = pl.BlockSpec(memory_space=pltpu.VMEM)
    sds = jax.ShapeDtypeStruct
    dma = pltpu.SemaphoreType.DMA
    column_map, output_full, hidden, attn_block, normed_s, query_rot, keys, values, mixed_s = (
        pl.pallas_call(
            partial(forward_kernel, (reps, shards, kv_start_of)),
            out_shape=(
                sds((d_s, block_width), BF16),
                sds((d_s, heads_s), BF16),
                sds((length, d_s), BF16),
                sds((per_block, length, wide_t), F32),
                sds((length, d_s), BF16),
                sds((length, heads_s), BF16),
                sds((length, kv_width), BF16),
                sds((length, kv_width), BF16),
                sds((length, heads_s), BF16),
            ),
            in_specs=[any_spec] * 2 + [vmem_spec] * 4 + [any_spec] * 9,
            out_specs=(any_spec,) * 5 + (vmem_spec,) * 4,
            scratch_shapes=[
                pltpu.VMEM((d_s, heads_s), BF16),
                pltpu.VMEM((d_s, kv_width), BF16),
                pltpu.VMEM((d_s, kv_width), BF16),
                pltpu.VMEM((d_s, heads_s), BF16),
                pltpu.VMEM((d_t, heads_t), BF16),
                pltpu.VMEM((d_t, kv_t), BF16),
                pltpu.VMEM((d_t, kv_t), BF16),
                pltpu.VMEM((d_t, heads_t), BF16),
                pltpu.VMEM((length, d_s), BF16),
                pltpu.VMEM((length, d_t), BF16),
                pltpu.VMEM((length, d_s), BF16),
                pltpu.VMEM((count_s, length, wide_s), BF16),
                pltpu.VMEM((count_s, length, wide_s), BF16),
                pltpu.VMEM((count_s, length, wide_s), BF16),
                pltpu.VMEM((length, heads_t), BF16),
                pltpu.VMEM((length, kv_t), BF16),
                pltpu.VMEM((length, kv_t), BF16),
                pltpu.VMEM((length, heads_t), BF16),
                pltpu.VMEM((per_block, length, wide_t), F32),
                pltpu.VMEM((most, length, wide_t), BF16),
                pltpu.VMEM((most, length, wide_t), BF16),
                dma((9, messages)),
                dma((9, messages)),
                dma((9,)),
                dma((2, count_s)),
                dma((2, count_s)),
                dma((2, most)),
                dma((2, most)),
                dma((7,)),
            ],
            compiler_params=pltpu.CompilerParams(
                collective_id=0, has_side_effects=True, vmem_limit_bytes=VMEM_BYTES
            ),
        )(
            student_states,
            teacher_states,
            student_gain.reshape(1, -1),
            teacher_gain.reshape(1, -1),
            cosine,
            sine,
            student_query,
            student_key,
            student_value,
            student_output,
            teacher_query,
            teacher_key,
            teacher_value,
            teacher_output,
            projection,
        )
    )
    attn_block = jnp.transpose(attn_block, (1, 0, 2)).reshape(length, block_width)
    own_states = lax.dynamic_slice_in_dim(teacher_states, shard_index * block_width, block_width, 1)
    teacher_hidden = own_states.astype(F32) + attn_block
    scaling = 1.0 / math.sqrt(reps * length)
    predicted = jnp.dot(hidden, column_map, preferred_element_type=F32)
    grad_pred = ((predicted - teacher_hidden) * scaling).astype(BF16)
    grad_hidden = pl.pallas_call(
        partial(gradient_kernel, (reps, shards)),
        out_shape=sds((length, d_s), BF16),
        in_specs=[vmem_spec, any_spec],
        out_specs=vmem_spec,
        scratch_shapes=[
            pltpu.VMEM((d_s, block_width), BF16),
            pltpu.VMEM((count_s, length, wide_s), BF16),
            pltpu.VMEM((count_s, length, wide_s), BF16),
            pltpu.VMEM((count_s, length, wide_s), BF16),
            dma((2, count_s)),
            dma((2, count_s)),
            dma((1,)),
        ],
        compiler_params=pltpu.CompilerParams(
            collective_id=1, has_side_effects=True, vmem_limit_bytes=VMEM_BYTES
        ),
    )(grad_pred, column_map)
    grad_mixed = jnp.dot(grad_hidden, output_full, preferred_element_type=F32)
    _, pullback = jax.vjp(
        partial(attend, keys=keys, values=values, head_dim=HD), query_rot.astype(F32)
    )
    grad_rot = pullback(grad_mixed)[0]
    grad_query = rotate(grad_rot, cosine, -sine).astype(BF16)
    out_term = jnp.dot(grad_hidden.T, mixed_s, preferred_element_type=F32)
    query_term = jnp.dot(normed_s.T, grad_query, preferred_element_type=F32)
    return (halving_scatter(query_term, "rep"), halving_scatter(out_term, "rep"))


def solution(mesh):
    return jax.shard_map(
        partial(local, mesh.shape["rep"], mesh.shape["shard"]),
        mesh=mesh,
        in_specs=(
            P("rep", None),
            P("rep", None),
            P(),
            P(),
            P("rep", "shard"),
            P("rep", "shard"),
            P("rep", "shard"),
            P("rep", "shard"),
            P("rep", "shard"),
            P("rep", None),
            P("rep", None),
            P("rep", "shard"),
            P("rep", "shard"),
        ),
        out_specs=(P("rep", "shard"), P("rep", "shard")),
        check_vma=False,
    )
```

profile of v0, /device:TPU:0, one launch (start us, length us, event | category | flops | bytes accessed | tf_op | source)
XLA Modules:
  0.0 370.2 jit_solution(765237762812779291)
XLA Ops:
  0.7 1.3 reshape.164.gain_s
  4.3 202.2 %shard_map.140 = (bf16[3584,1280]{1,0:T(8,128)(2,1)}, bf16[3584,512]{1,0:T(8,128)(2,1)}, bf16[384,3584]{1,0:T(8,128)(2,1)}, f32[5,384,256]{2,1,0:T(8,128)}, bf16...) custom-call(bf16[384,3584]{1,0:T(8,128)(2,1)} %states_s.1, ...), custom_call_target="tpu_custom_call" | custom-call | tf_op jit(solution)/shard_map/pallas_call | solution.py:677
  206.5 1.9 copy.27
  208.4 1.9 copy.28
  210.2 9.9 %fusion.1.grad_pred = bf16[384,1280]{1,0:T(8,128)(2,1)} fusion(bf16[384,3584]{1,0:T(8,128)(2,1)} %get-tuple-element.12, bf16[3584,1280]{1,0:T(8,128)(2,1)} %get-tuple-element.13.column_map, f32[384,1280]{1,0:T(8,128)} %copy.28, bf16[384,5120]{1,0:T(8,128)(2,1)} %states_t.1, s32[]{:T(128)S(6)} %select_n.51), kind=kOutput, calls=%fused_computation.4 | convolution fusion | flops 3525672960 | bytes 15859716 | tf_op jit(solution)/shard_map/dot_general | solution.py:748
  220.2 82.9 %shard_map.141 = bf16[384,3584]{1,0:T(8,128)(2,1)} custom-call(bf16[384,1280]{1,0:T(8,128)(2,1)} %fusion.1.grad_pred, bf16[3584,1280]{1,0:T(8,128)(2,1)} %get-tuple-element.13.column_map), custom_call_target="tpu_custom_call" | custom-call | tf_op jit(solution)/shard_map/pallas_call | solution.py:750
  303.1 1.7 fusion.55
  305.2 4.2 %fusion.56 = bf16[384,512]{0,1:T(8,128)(2,1)S(1)} fusion(bf16[384,3584]{1,0:T(8,128)(2,1)S(1)} %copy-done, bf16[3584,512]{1,0:T(8,128)(2,1)} %get-tuple-element.15), kind=kOutput, calls=%fused_computation.97 | convolution fusion | flops 1409286144 | bytes 6815744 | tf_op jit(solution)/shard_map/transpose(jvp())/reshape | solution.py:61
  311.2 1.3 fusion.18
  312.8 1.5 copy-done.6
  314.3 2.1 fusion.57
  316.5 3.5 fusion.53
  320.0 2.6 fusion.25
  322.5 2.5 fusion.27
  325.6 2.1 fusion.58
  331.6 2.3 bitcast_add_fusion.3
  334.9 1.5 bitcast_add_fusion.2
  339.2 1.2 collective-permute-start.10
  340.4 7.0 %collective-permute-done.1 = bf16[2,448,256]{2,1,0:T(8,128)(2,1)S(1)} collective-permute-done((bf16[2,448,256]{2,1,0:T(8,128)(2,1)S(1)}, bf16[2,448,256]{2,1,0:T(8,128)(2,1)S(1)}, u32[]{:S(2)}, u32[]{:S(2)}) %collective-permute-start.1) | collective-permute-done | bytes 458784 | tf_op jit(solution)/shard_map/ppermute | solution.py:81
  348.5 1.5 collective-permute-done.4
  351.2 6.0 %collective-permute-done.7 = bf16[2,448,256]{2,1,0:T(8,128)(2,1)S(1)} collective-permute-done((bf16[2,448,256]{2,1,0:T(8,128)(2,1)S(1)}, bf16[2,448,256]{2,1,0:T(8,128)(2,1)S(1)}, u32[]{:S(2)}, u32[]{:S(2)}) %collective-permute-start.7) | collective-permute-done | bytes 458784 | tf_op jit(solution)/shard_map/ppermute | solution.py:81
  358.3 1.4 collective-permute-done.10
  361.1 3.6 collective-permute-done.2
  365.9 3.1 collective-permute-done.8
  (75 shorter events, 19.7 us)
Async XLA Ops:
  3.6 0.7 copy-start.7
  220.2 82.9 %copy-start.9 = (bf16[384,128]{1,0:T(8,128)(2,1)S(1)}, bf16[384,128]{1,0:T(8,128)(2,1)}, u32[]{:S(2)}) copy-start(bf16[384,128]{1,0:T(8,128)(2,1)} %get-tuple-element.17) | copy-start | bytes 294916
  303.1 2.1 copy-start
  305.2 4.2 %copy-start.10 = (bf16[384,128]{1,0:T(8,128)(2,1)S(1)}, bf16[384,128]{1,0:T(8,128)(2,1)}, u32[]{:S(2)}) copy-start(bf16[384,128]{1,0:T(8,128)(2,1)} %get-tuple-element.16) | copy-start | bytes 294916
  312.5 1.8 copy-start.6
  320.0 5.6 %copy-start.8 = (bf16[384,512]{1,0:T(8,128)(2,1)S(1)}, bf16[384,512]{1,0:T(8,128)(2,1)}, u32[]{:S(2)}) copy-start(bf16[384,512]{1,0:T(8,128)(2,1)} %get-tuple-element.19) | copy-start | bytes 1179652
  322.5 9.0 %collective-permute-start = (bf16[2,2,448,256]{3,2,0,1:T(8,128)(2,1)}, bf16[2,2,448,256]{3,2,0,1:T(8,128)(2,1)}, u32[]{:S(2)}, u32[]{:S(2)}) collective-permute-start(bf16[2,2,448,256]{3,2,0,1:T(8,128)(2,1)} %fusion.25), channel_id=1, source_target_pairs={{0,4},{4,0},{8,12},{12,8},{16,20},{20,16},{24,28},{28,24},{1,5},{5... | collective-permute-start | bytes 2752520 | tf_op jit(solution)/shard_map/ppermute | solution.py:81
  325.1 9.8 %collective-permute-start.3 = (bf16[2,2,448,256]{3,2,1,0:T(8,128)(2,1)}, bf16[2,2,448,256]{3,2,1,0:T(8,128)(2,1)}, u32[]{:S(2)}, u32[]{:S(2)}) collective-permute-start(bf16[2,2,448,256]{3,2,1,0:T(8,128)(2,1)} %fusion.27), channel_id=1, source_target_pairs={{0,4},{4,0},{8,12},{12,8},{16,20},{20,16},{24,28},{28,24},{1,5},{5... | collective-permute-start | bytes 2752520 | tf_op jit(solution)/shard_map/ppermute | solution.py:81
  328.3 2.1 copy-start.1
  328.3 3.3 copy-start.4
  329.4 8.0 %collective-permute-start.6 = (bf16[2,2,448,256]{3,2,0,1:T(8,128)(2,1)}, bf16[2,2,448,256]{3,2,0,1:T(8,128)(2,1)S(1)}, u32[]{:S(2)}, u32[]{:S(2)}) collective-permute-start(bf16[2,2,448,256]{3,2,0,1:T(8,128)(2,1)} %fusion.26), channel_id=1, source_target_pairs={{0,4},{4,0},{8,12},{12,8},{16,20},{20,16},{24,28},{28,24},{1,5},{5... | collective-permute-start | bytes 2752520 | tf_op jit(solution)/shard_map/ppermute | solution.py:81
  331.6 7.3 %collective-permute-start.9 = (bf16[2,2,448,256]{3,2,1,0:T(8,128)(2,1)S(1)}, bf16[2,2,448,256]{3,2,1,0:T(8,128)(2,1)S(1)}, u32[]{:S(2)}, u32[]{:S(2)}) collective-permute-start(bf16[2,2,448,256]{3,2,1,0:T(8,128)(2,1)S(1)} %fusion.28), channel_id=1, source_target_pairs={{0,4},{4,0},{8,12},{12,8},{16,20},{20,16},{24,28},{28,24},{1,5},{5... | collective-permute-start | bytes 2752520 | tf_op jit(solution)/shard_map/ppermute | solution.py:81
  331.6 3.3 copy-start.3
  334.0 3.5 copy-start.5
  334.0 13.5 %collective-permute-start.1 = (bf16[2,448,256]{2,1,0:T(8,128)(2,1)S(1)}, bf16[2,448,256]{2,1,0:T(8,128)(2,1)S(1)}, u32[]{:S(2)}, u32[]{:S(2)}) collective-permute-start(bf16[2,448,256]{2,1,0:T(8,128)(2,1)S(1)} %fusion.33), channel_id=1, source_target_pairs={{0,8},{4,12},{8,0},{12,4},{16,24},{20,28},{24,16},{28,20},{1,9},{5... | collective-permute-start | bytes 1376264 | tf_op jit(solution)/shard_map/ppermute | solution.py:81
  336.5 2.4 copy-start.2
  336.5 13.5 %collective-permute-start.4 = (bf16[2,448,256]{2,1,0:T(8,128)(2,1)S(1)}, bf16[2,448,256]{2,1,0:T(8,128)(2,1)S(1)}, u32[]{:S(2)}, u32[]{:S(2)}) collective-permute-start(bf16[2,448,256]{2,1,0:T(8,128)(2,1)S(1)} %fusion.34), channel_id=1, source_target_pairs={{0,16},{4,20},{8,24},{12,28},{16,0},{20,4},{24,8},{28,12},{1,17},{... | collective-permute-start | bytes 1376264 | tf_op jit(solution)/shard_map/ppermute | solution.py:81
  337.8 19.5 %collective-permute-start.7 = (bf16[2,448,256]{2,1,0:T(8,128)(2,1)S(1)}, bf16[2,448,256]{2,1,0:T(8,128)(2,1)S(1)}, u32[]{:S(2)}, u32[]{:S(2)}) collective-permute-start(bf16[2,448,256]{2,1,0:T(8,128)(2,1)S(1)} %fusion.35), channel_id=1, source_target_pairs={{0,8},{4,12},{8,0},{12,4},{16,24},{20,28},{24,16},{28,20},{1,9},{5... | collective-permute-start | bytes 1376264 | tf_op jit(solution)/shard_map/ppermute | solution.py:81
  339.2 20.6 %collective-permute-start.10 = (bf16[2,448,256]{2,1,0:T(8,128)(2,1)S(1)}, bf16[2,448,256]{2,1,0:T(8,128)(2,1)S(1)}, u32[]{:S(2)}, u32[]{:S(2)}) collective-permute-start(bf16[2,448,256]{2,1,0:T(8,128)(2,1)S(1)} %fusion.36), channel_id=1, source_target_pairs={{0,16},{4,20},{8,24},{12,28},{16,0},{20,4},{24,8},{28,12},{1,17},{... | collective-permute-start | bytes 1376264 | tf_op jit(solution)/shard_map/ppermute | solution.py:81
  347.6 17.1 %collective-permute-start.2 = (bf16[448,256]{1,0:T(8,128)(2,1)S(1)}, bf16[448,256]{1,0:T(8,128)(2,1)S(1)}, u32[]{:S(2)}, u32[]{:S(2)}) collective-permute-start(bf16[448,256]{1,0:T(8,128)(2,1)S(1)} %fusion.39), channel_id=1, source_target_pairs={{0,16},{4,20},{8,24},{12,28},{16,0},{20,4},{24,8},{28,12},{1,17},{... | collective-permute-start | bytes 688136 | tf_op jit(solution)/shard_map/ppermute | solution.py:81
  350.1 14.7 %collective-permute-start.5 = (bf16[448,256]{1,0:T(8,128)(2,1)S(1)}, bf16[448,256]{1,0:T(8,128)(2,1)S(1)}, u32[]{:S(2)}, u32[]{:S(2)}) collective-permute-start(bf16[448,256]{1,0:T(8,128)(2,1)S(1)} %fusion.40), channel_id=1, source_target_pairs={{0,8},{4,12},{8,0},{12,4},{16,24},{20,28},{24,16},{28,20},{1,9},{5... | collective-permute-start | bytes 688136 | tf_op jit(solution)/shard_map/ppermute | solution.py:81
  357.4 11.6 %collective-permute-start.8 = (bf16[448,256]{1,0:T(8,128)(2,1)S(1)}, bf16[448,256]{1,0:T(8,128)(2,1)S(1)}, u32[]{:S(2)}, u32[]{:S(2)}) collective-permute-start(bf16[448,256]{1,0:T(8,128)(2,1)S(1)} %fusion.41), channel_id=1, source_target_pairs={{0,16},{4,20},{8,24},{12,28},{16,0},{20,4},{24,8},{28,12},{1,17},{... | collective-permute-start | bytes 688136 | tf_op jit(solution)/shard_map/ppermute | solution.py:81
  359.9 9.1 %collective-permute-start.11 = (bf16[448,256]{1,0:T(8,128)(2,1)S(1)}, bf16[448,256]{1,0:T(8,128)(2,1)S(1)}, u32[]{:S(2)}, u32[]{:S(2)}) collective-permute-start(bf16[448,256]{1,0:T(8,128)(2,1)S(1)} %fusion.42), channel_id=1, source_target_pairs={{0,8},{4,12},{8,0},{12,4},{16,24},{20,28},{24,16},{28,20},{1,9},{5... | collective-permute-start | bytes 688136 | tf_op jit(solution)/shard_map/ppermute | solution.py:81
where the time goes:
time: 371 us; the launch traced here: 370 us
  Pallas kernels  285 us (77%)
  waiting for transfers between devices  22.8 us (6%)
  matrix products  22.1 us (6%)
  local copies, waits for them, and re-layouts  20.2 us (5%)
  other arithmetic  10.3 us (3%)
  starting transfers between devices  8.82 us (2%)
    pallas_call x1, Pallas kernels, local(): pl.pallas_call(partial(forward_kernel, (reps, shards, kv_start_of)), out_...  202 us
    pallas_call x1, Pallas kernels, local(): pl.pallas_call(partial(gradient_kernel, (reps, shards)), out_shape=sds((l...  82.9 us
    ppermute x12, waiting for transfers between devices, halving_scatter(): lax.ppermute(sent.astype(BF16), axis, [(i, i ^ 1 << bit) for i in range(c...  22.8 us
    dot_general x1, matrix products, local(): predicted = jnp.dot(hidden, column_map, preferred_element_type=F32)  9.91 us
    ppermute x12, starting transfers between devices, halving_scatter(): lax.ppermute(sent.astype(BF16), axis, [(i, i ^ 1 << bit) for i in range(c...  8.82 us
  transfers between devices with their start and end apart: 12, of which 6 were waited for; matrix products, arithmetic and copies ran while one was open for 3% of the time, Pallas kernels for 0%

commit v1 on v0

--- a/solution.py
+++ b/solution.py
@@ -3,6 +3,7 @@
 
 import jax
 import jax.numpy as jnp
+import numpy as np
 from jax import lax
 from jax.experimental import pallas as pl
 from jax.experimental.pallas import tpu as pltpu
@@ -17,73 +18,21 @@
 
 F32 = jnp.float32
 BF16 = jnp.bfloat16
-VMEM_BYTES = 66 * 1000 * 1000
+VMEM_BYTES = 67_000_000
 LAG = 2
 
 
 def tables(length):
     halfway = HD // 2
-    inverse = theta_base ** (-(jnp.arange(halfway, dtype=F32) * 2.0 / HD))
-    angles = jnp.arange(length, dtype=F32)[:, None] * inverse[None, :]
-    cosine = jnp.cos(angles)
-    sine = jnp.sin(angles)
+    inverse = theta_base ** (-(np.arange(halfway) * 2.0 / HD))
+    inverse = inverse.astype(np.float32)
+    angles = np.arange(length, dtype=np.float32)[:, None] * inverse[None, :]
+    cosine = np.cos(angles)
+    sine = np.sin(angles)
     return (
-        jnp.concatenate([cosine, cosine], axis=1),
-        jnp.concatenate([-sine, sine], axis=1),
+        np.concatenate([cosine, cosine], axis=1).astype(np.float32),
+        np.concatenate([-sine, sine], axis=1).astype(np.float32),
     )
-
-
-def rotate(values, cosine, sine):
-    length = values.shape[0]
-    split = values.reshape(length, -1, HD)
-    swapped = jnp.roll(split, HD // 2, axis=-1)
-    turned = split * cosine[:, None, :] + swapped * sine[:, None, :]
-    return turned.reshape(length, -1)
-
-
-def attend(query_rot, keys, values, head_dim):
-    length = query_rot.shape[0]
-    kv_heads = keys.shape[1] // head_dim
-    group_size = query_rot.shape[1] // head_dim // kv_heads
-    queries = query_rot.astype(BF16).reshape(length, kv_heads, group_size, head_dim)
-    key_heads = keys.reshape(length, kv_heads, head_dim)
-    value_heads = values.reshape(length, kv_heads, head_dim)
-    scores = jnp.einsum(
-        "qkgd,skd->kgqs", queries, key_heads, preferred_element_type=F32
-    ) * head_dim ** (-0.5)
-    rows_index = jnp.arange(length)[:, None]
-    column_index = jnp.arange(length)[None, :]
-    scores = jnp.where(rows_index >= column_index, scores, -1e30)
-    highest = jnp.max(scores, axis=-1, keepdims=True)
-    weights = jnp.exp(scores - highest)
-    probs = (weights / jnp.sum(weights, axis=-1, keepdims=True)).astype(BF16)
-    mixed = jnp.einsum("kgqs,skd->qkgd", probs, value_heads, preferred_element_type=F32)
-    return mixed.reshape(length, -1)
-
-
-def halving_scatter(term, axis):
-    count = lax.axis_size(axis)
-    bits = count.bit_length() - 1
-    here = lax.axis_index(axis)
-    rows = term.shape[0] // count
-    width = term.shape[1] // 2
-    outs = []
-    for half in range(2):
-        part = term[:, half * width : (half + 1) * width].reshape((2,) * bits + (rows, width))
-        left = list(range(bits - 1, -1, -1))
-        order = [0] + (list(range(1, bits)) if half == 0 else list(range(bits - 1, 0, -1)))
-        for bit in order:
-            place = left.index(bit)
-            left.remove(bit)
-            mine = lax.rem(lax.div(here, 2**bit), 2)
-            sent = lax.dynamic_index_in_dim(part, 1 - mine, place, keepdims=False)
-            kept = lax.dynamic_index_in_dim(part, mine, place, keepdims=False)
-            came = lax.ppermute(
-                sent.astype(BF16), axis, [(i, i ^ (1 << bit)) for i in range(count)]
-            )
-            part = kept.astype(F32) + came.astype(F32)
-        outs.append(part)
-    return jnp.concatenate(outs, axis=1)
 
 
 def tile_of(width):
@@ -92,6 +41,14 @@
 
 def dot_nt(left, right):
     return lax.dot_general(left, right, (((1,), (1,)), ((), ())), preferred_element_type=F32)
+
+
+def dot_tn(left, right):
+    return lax.dot_general(left, right, (((0,), (0,)), ((), ())), preferred_element_type=F32)
+
+
+def span(index, size):
+    return pl.ds(pl.multiple_of(index * size, size), size)
 
 
 class Place:
@@ -229,7 +186,8 @@
             action()
 
 
-def line_sum(place, count, produce, consume, own, rightward, leftward, send_sem, recv_sem, hooks):
+def line_sum(place, count, produce, consume, own, rightward, leftward, send_sem, recv_sem, hooks,
+             done_hooks=()):
     z = place.z
     ends = place.shards - 1
     waves = count + LAG * ends
@@ -285,12 +243,14 @@
         def _():
             total = rightward[final].astype(F32) + leftward[final].astype(F32)
             consume(final, total - own[final].astype(F32))
+            run_hooks(done_hooks, final, count)
 
         run_hooks(hooks, w, waves)
         return carry
 
     lax.fori_loop(0, waves, wave_body, 0)
     late_hooks(hooks, waves)
+    late_hooks(done_hooks, count)
 
     def drain(j, carry):
         for way in range(2):
@@ -373,6 +333,99 @@
             lax.fori_loop(0, (ends - line) * per_block, drain, 0)
 
     return finish
+
+
+class RingScatter:
+    def __init__(self, place, partial_sums, pair, ring, out, index, pair_sems, ring_sems):
+        self.place = place
+        self.partial = partial_sums
+        self.pair = pair
+        self.ring = ring
+        self.out = out
+        self.index = index
+        self.pair_sems = pair_sems
+        self.ring_sems = ring_sems
+        self.half = place.chips // 2
+        self.rows = out.shape[0]
+        self.steps = ring_order(place.chips)
+
+    def exchange(self, i):
+        self.pair_copy(i).start()
+
+    def pair_copy(self, i):
+        owner = self.place.rep_at(self.steps[i], 1 - self.place.core)
+        return pltpu.make_async_remote_copy(
+            src_ref=self.partial.at[span(owner, self.rows)],
+            dst_ref=self.pair(i),
+            send_sem=self.pair_sems[0].at[self.index, i],
+            recv_sem=self.pair_sems[1].at[self.index, i],
+            device_id={"rep": self.place.partner},
+        )
+
+    def message(self, step, part):
+        return 0 if step == self.half else 1 + 2 * (self.half - 1 - step) + part
+
+    def half_of(self, ref, part):
+        return ref.at[pl.ds(part * (self.rows // 2), self.rows // 2)]
+
+    def ring_copy(self, way, step, part, i):
+        m = self.message(step, part)
+        return pltpu.make_async_remote_copy(
+            src_ref=self.half_of(self.pair(i), part),
+            dst_ref=self.ring.at[way, m],
+            send_sem=self.ring_sems[0].at[self.index, way, m],
+            recv_sem=self.ring_sems[1].at[self.index, way, m],
+            device_id={"rep": (self.place.right, self.place.left)[way]},
+        )
+
+    def moves(self, i):
+        e, h = self.steps[i], self.half
+        if e == h:
+            return [(way, h, way, False) for way in range(2)]
+        way, step = (0, e) if e > 0 else (1, -e)
+        return [(way, step, part, part == way or step + 1 < h) for part in range(2)]
+
+    def fresh(self, i, part):
+        owner = self.place.rep_at(self.steps[i], self.place.core)
+        rows = self.rows // 2
+        mine = self.partial[span(2 * owner + part, rows), :].astype(F32)
+        return mine + self.half_of(self.pair(i), part)[...].astype(F32)
+
+    def incoming(self, way, step, part, i):
+        self.ring_copy(way, step, part, i).wait_recv()
+        return self.ring[way, self.message(step, part)].astype(F32)
+
+    def forward(self, i):
+        self.pair_copy(i).wait_recv()
+        if self.steps[i] != 0:
+            for way, step, part, has in self.moves(i):
+                value = self.fresh(i, part)
+                if has:
+                    value = value + self.incoming(way, step + 1, part, i)
+                self.half_of(self.pair(i), part)[...] = value.astype(BF16)
+                self.ring_copy(way, step, part, i).start()
+            return
+        for part in range(2):
+            value = self.fresh(i, part)
+            for way in range(2):
+                if part == way or self.half > 1:
+                    value = value + self.incoming(way, 1, part, i)
+            self.half_of(self.out, part)[...] = value
+
+    def drain(self):
+        for i, e in enumerate(self.steps):
+            self.pair_copy(i).wait_send()
+            if e != 0:
+                for way, step, part, _ in self.moves(i):
+                    self.ring_copy(way, step, part, i).wait_send()
+
+
+def ring_order(chips):
+    half = chips // 2
+    order = [half]
+    for step in range(half - 1, 0, -1):
+        order += [step, -step]
+    return order + [0]
 
 
 def normalise(states, gain, block=16):
@@ -432,7 +485,19 @@
     lax.fori_loop(first, first + count, body, 0)
 
 
-def forward_kernel(
+def backward_head(h, query, keys, values, grad_mixed, grad_query, cosine, sine, group):
+    at = span(h, HD)
+    kv = span(lax.div(h, group), HD)
+    probs = soft(masked_scores(query[:, at], keys[:, kv]))
+    grad_probs = dot_nt(grad_mixed[:, at].astype(BF16), values[:, kv]).astype(BF16).astype(F32)
+    inner = jnp.sum(grad_probs * probs, axis=-1, keepdims=True)
+    grad_scores = probs * (grad_probs - inner) * HD ** (-0.5)
+    grad_rot = jnp.dot(grad_scores.astype(BF16), keys[:, kv], preferred_element_type=F32)
+    grad_rot = grad_rot.astype(BF16).astype(F32)
+    grad_query[:, at] = turned(grad_rot, cosine[...], -sine[...]).astype(BF16)
+
+
+def step_kernel(
     sizes,
     states_s,
     states_t,
@@ -450,14 +515,8 @@
     w_to,
     w_pj,
     map_full,
-    output_full,
-    hidden_out,
-    attn_out,
-    normed_out,
-    query_s,
-    key_s,
-    value_s,
-    mixed_s,
+    query_grad,
+    output_grad,
     sq,
     sk,
     sv,
@@ -472,6 +531,10 @@
     own_s,
     right_s,
     left_s,
+    query_s,
+    key_s,
+    value_s,
+    mixed_s,
     query_t,
     key_t,
     value_t,
@@ -479,17 +542,28 @@
     attn_t,
     right_t,
     left_t,
+    grad_mixed,
+    ring_out,
+    ring_query,
     gather_send,
     gather_recv,
     gather_local,
     sum_send,
     sum_recv,
+    back_send,
+    back_recv,
     scatter_send,
     scatter_recv,
+    pair_send,
+    pair_recv,
+    ring_send,
+    ring_recv,
     copies,
+    map_sems,
 ):
     reps, shards, kv_start_of = sizes
     place = Place(reps, shards)
+    length = normed_s.shape[0]
     kv_width = sk.shape[1]
     kv_at = pl.ds(pl.multiple_of(kv_start_of(place.z), HD), kv_width)
     sources = (w_sq, w_sk.at[:, kv_at], w_sv.at[:, kv_at], w_so, w_tq, w_tk, w_tv, w_to, w_pj)
@@ -499,8 +573,14 @@
         for i, (source, full) in enumerate(zip(sources, fulls))
     ]
     half = place.chips // 2
-    groups = {"P0": weights[0:3], "P1": weights[3:4], "P2a": weights[5:7], "P2b": weights[4:5],
-              "P3": weights[7:8], "P4": weights[8:9]}
+    groups = {
+        "P0": weights[0:3],
+        "P1": weights[3:4],
+        "P2a": weights[5:7],
+        "P2b": weights[4:5],
+        "P3": weights[7:8],
+        "P4": weights[8:9],
+    }
 
     def start(name):
         for weight in groups[name]:
@@ -515,6 +595,11 @@
             relay(name, step)
         for weight in groups[name]:
             weight.finish()
+
+    def drain(names):
+        for name in names:
+            for weight in groups[name]:
+                weight.drain()
 
     in_s = pltpu.make_async_copy(states_s, normed_s, copies.at[0])
     in_h = pltpu.make_async_copy(states_s, hidden, copies.at[1])
@@ -536,26 +621,27 @@
     project(normed_s, sk, key_s, cosine, sine, 0, kv_width // kv_tile, kv_tile)
     project(normed_s, sv, value_s, None, None, 0, kv_width // kv_tile, kv_tile)
     project(normed_s, sq, query_s, cosine, sine, 0, sq.shape[1] // tile, tile)
-    out_n = pltpu.make_async_copy(normed_s, normed_out, copies.at[3])
-    out_n.start()
     relay("P1", 1)
     start("P2a")
     start("P2b")
     heads = sq.shape[1] // HD
-    attention(query_s, key_s, value_s, mixed_s, 0, heads, heads // (kv_width // HD))
+    group = heads // (kv_width // HD)
+    attention(query_s, key_s, value_s, mixed_s, 0, heads, group)
     finish("P1")
-    out_o = pltpu.make_async_copy(so, output_full, copies.at[4])
-    out_o.start()
     in_h.wait()
 
-    width = own_s.shape[2]
+    count, _, width = own_s.shape
+    block_width = map_full.shape[1]
+    states_at = pl.ds(pl.multiple_of(place.z * block_width, 128), block_width)
+    in_b = pltpu.make_async_copy(
+        states_t.at[:, states_at], normed_t.at[:, 0:block_width], copies.at[3]
+    )
 
     def produce_s(j):
-        rows = pl.ds(pl.multiple_of(j * width, width), width)
-        return dot_nt(mixed_s[...], so[rows, :])
+        return dot_nt(mixed_s[...], so[span(j, width), :])
 
     def consume_s(j, total):
-        at = pl.ds(pl.multiple_of(j * width, width), width)
+        at = span(j, width)
         hidden[:, at] = (hidden[:, at].astype(F32) + total).astype(BF16)
 
     t_tile = tile_of(tq.shape[1])
@@ -563,72 +649,170 @@
     t_heads = tq.shape[1] // HD
     t_group = t_heads // (tk.shape[1] // HD)
     hooks = [
-        (2, lambda: relay("P2a", 1)),
-        (7, lambda: relay("P2b", 1)),
-        (7, lambda: start("P3")),
-        (9, lambda: finish("P2a")),
-        (11, lambda: finish("P2b")),
+        (5, lambda: relay("P2a", 1)),
+        (14, lambda: relay("P2b", 1)),
+        (14, lambda: start("P3")),
+        (17, lambda: finish("P2a")),
+        (22, lambda: finish("P2b")),
     ]
-    wave = 11
+    wave = 22
     for t in range(tk.shape[1] // t_kv):
         hooks.append((wave, partial(project, normed_t, tk, key_t, cosine, sine, t, 1, t_kv)))
+        wave += 1
         hooks.append((wave, partial(project, normed_t, tv, value_t, None, None, t, 1, t_kv)))
         wave += 1
     for t in range(tq.shape[1] // t_tile):
         hooks.append((wave, partial(project, normed_t, tq, query_t, cosine, sine, t, 1, t_tile)))
         wave += 1
-    hooks.append((wave, lambda: relay("P3", 1)))
-    hooks.append((wave, lambda: start("P4")))
+    hooks.append((wave, lambda: drain(("P0", "P1", "P2a", "P2b"))))
+    hooks.append((wave, in_b.start))
     for h in range(t_heads):
         hooks.append((wave, partial(attention, query_t, key_t, value_t, mixed_t, h, 1, t_group)))
-        wave += h % 2
+        wave += 1
+    hooks.append((wave - 2, lambda: relay("P3", 1)))
+    hooks.append((wave - 2, lambda: start("P4")))
     drain_s = line_sum(
-        place, own_s.shape[0], produce_s, consume_s, own_s, right_s, left_s, sum_send, sum_recv, hooks
+        place, count, produce_s, consume_s, own_s, right_s, left_s, sum_send, sum_recv, hooks
     )
-    out_h = pltpu.make_async_copy(hidden, hidden_out, copies.at[5])
-    out_h.start()
+    drain_s()
     finish("P3")
 
-    width_t = attn_t.shape[2]
+    per_block, _, width_t = attn_t.shape
+    in_b.wait()
 
     def produce_t(j):
-        rows = pl.ds(pl.multiple_of(j * width_t, width_t), width_t)
-        return dot_nt(mixed_t[...], to[rows, :])
-
+        return dot_nt(mixed_t[...], to[span(j, width_t), :])
+
+    columns = (tk, tv)
+
+    def column_copy(t):
+        return pltpu.make_async_copy(
+            map_full.at[:, t * width_t : (t + 1) * width_t],
+            columns[t % 2].at[0 : map_full.shape[0]],
+            map_sems.at[t % 2],
+        )
+
+    def first_columns():
+        for t in range(min(2, per_block)):
+            column_copy(t).start()
+
+    def predict(t):
+        column_copy(t).wait()
+        product = jnp.dot(
+            hidden[...], columns[t % 2][0 : map_full.shape[0]], preferred_element_type=F32
+        )
+        at = pl.ds(t * width_t, width_t)
+        attn_t[t] += normed_t[:, at].astype(F32) - product
+        if t + 2 < per_block:
+            column_copy(t + 2).start()
+
+    hooks = [(2, lambda: relay("P4", 1)), (8, lambda: finish("P4")), (8, first_columns)]
+    hooks += [(9 + t, partial(predict, t)) for t in range(per_block)]
     drain_t = line_scatter(
-        place, attn_t.shape[0], produce_t, attn_t, right_t, left_t, scatter_send, scatter_recv,
-        [(3, lambda: relay("P4", 1)), (9, lambda: finish("P4"))],
+        place, per_block, produce_t, attn_t, right_t, left_t, scatter_send, scatter_recv, hooks
     )
-    out_a = pltpu.make_async_copy(attn_t, attn_out, copies.at[6])
-    out_a.start()
-    drain_s()
+    scaling = 1.0 / math.sqrt(reps * length)
+    grad_pred = normed_t.at[:, 0:block_width]
+    for t in range(per_block):
+        grad_pred[:, t * width_t : (t + 1) * width_t] = (attn_t[t] * -scaling).astype(BF16)
+
+    rows = query_grad.shape[0]
+    wide = query_grad.shape[1]
+    pair_sems = (pair_send, pair_recv)
+    ring_sems = (ring_send, ring_recv)
+
+    def slot(first):
+        return lambda i: tq.at[(first + i) * rows : (first + i + 1) * rows, 0:wide]
+
+    out_sum = RingScatter(
+        place, sq, slot(0), ring_out, output_grad, 0, pair_sems, ring_sems
+    )
+    query_sum = RingScatter(
+        place, so, slot(place.chips), ring_query, query_grad, 1, pair_sems, ring_sems
+    )
+    steps = ring_order(place.chips)
+    per_chip = count // place.chips
+    in_order = per_chip * place.chips == count
+
+    def tile_at(j):
+        if not in_order:
+            return j
+        turn = lax.div(j, per_chip)
+        chip = 0
+        for i, step in enumerate(steps):
+            chip = chip + jnp.where(turn == i, lax.div(place.rep_at(step, 0), 2), 0)
+        return chip * per_chip + lax.rem(j, per_chip)
+
+    slots = length // width
+
+    def rows_copy(j):
+        slot_at = lax.rem(j, slots)
+        return pltpu.make_async_copy(
+            map_full.at[span(tile_at(j), width)],
+            normed_t.at[span(slot_at, width), block_width : 2 * block_width],
+            map_sems.at[2 + slot_at],
+        )
+
+    def produce_b(j):
+        rows_copy(j).wait()
+        at = span(lax.rem(j, slots), width)
+        product = dot_nt(grad_pred[...], normed_t[at, block_width : 2 * block_width])
+
+        @pl.when(j + slots < count)
+        def _():
+            rows_copy(j + slots).start()
+
+        return product
+
+    grad_mixed[...] = jnp.zeros_like(grad_mixed)
+
+    def consume_b(j, total):
+        at = span(tile_at(j), width)
+        grad = total.astype(BF16)
+        grad_mixed[...] += jnp.dot(grad, so[at, :], preferred_element_type=F32)
+        sq[at, :] = dot_tn(grad, mixed_s[...]).astype(BF16)
+
+    for j in range(min(slots, count)):
+        rows_copy(j).start()
+    done = []
+    for i in range(place.chips):
+        ready = (i + 1) * per_chip - 1 if in_order else count
+        done.append((ready, partial(out_sum.exchange, i)))
+        done.append((ready + 3 if in_order else count, partial(out_sum.forward, i)))
+    drain_b = line_sum(
+        place, count, produce_b, consume_b, own_s, right_s, left_s, back_send, back_recv, [], done
+    )
+    grad_query = query_t.at[:, 0:wide]
+
+    def one_head(h, carry):
+        backward_head(h, query_s, key_s, value_s, grad_mixed, grad_query, cosine, sine, group)
+        return carry
+
+    lax.fori_loop(0, heads, one_head, 0)
+
+    def query_tile(t, carry):
+        so[span(t, width), :] = dot_tn(normed_s[:, span(t, width)], grad_query[...]).astype(BF16)
+        return carry
+
+    if in_order:
+        for i, step in enumerate(steps):
+            first = lax.div(place.rep_at(step, 0), 2) * per_chip
+            lax.fori_loop(first, first + per_chip, query_tile, 0)
+            query_sum.exchange(i)
+            if i > 0:
+                query_sum.forward(i - 1)
+        query_sum.forward(len(steps) - 1)
+    else:
+        lax.fori_loop(0, count, query_tile, 0)
+        for i in range(len(steps)):
+            query_sum.exchange(i)
+        for i in range(len(steps)):
+            query_sum.forward(i)
     drain_t()
-    for weight in weights:
-        weight.drain()
-    for copy in (out_n, out_o, out_h, out_a):
-        copy.wait()
-
-
-def gradient_kernel(
-    sizes, grad_pred, column_map, hidden_out, map_all, own, right, left, sum_send, sum_recv, copies
-):
-    reps, shards = sizes
-    place = Place(reps, shards)
-    inward = pltpu.make_async_copy(column_map, map_all, copies.at[0])
-    inward.start()
-    place.barrier(False, True)
-    inward.wait()
-    width = own.shape[2]
-
-    def produce(j):
-        rows = pl.ds(pl.multiple_of(j * width, width), width)
-        return dot_nt(grad_pred[...], map_all[rows, :])
-
-    def consume(j, total):
-        at = pl.ds(pl.multiple_of(j * width, width), width)
-        hidden_out[:, at] = total.astype(BF16)
-
-    line_sum(place, own.shape[0], produce, consume, own, right, left, sum_send, sum_recv, [])()
+    drain_b()
+    drain(("P3", "P4"))
+    out_sum.drain()
+    query_sum.drain()
 
 
 def local(
@@ -648,10 +832,10 @@
     student_output,
     projection,
 ):
-    shard_index = lax.axis_index("shard")
     length, d_t = teacher_states.shape
-    d_s = student_states.shape[1]
-    local_heads = student_query.shape[1] // HD
+    rows, heads_s = student_query.shape
+    d_s = rows * reps
+    local_heads = heads_s // HD
     group_size = HQ_S // KV_S
     kv_width = max(local_heads // group_size, 1) * HD
 
@@ -659,121 +843,100 @@
         return lax.div(z * local_heads, group_size) * HD
 
     cosine, sine = tables(length)
-    heads_s = student_query.shape[1]
     heads_t = teacher_query.shape[1]
     kv_t = teacher_key.shape[1]
     block_width = projection.shape[1]
-    wide_s = tile_of(d_s)
+    wide_s = 128
     wide_t = tile_of(block_width)
     count_s = d_s // wide_s
     per_block = block_width // wide_t
     most = (shards - 1) * per_block
-    messages = 4 * (reps // 4) + 1
+    chips = reps // 2
+    messages = 4 * (chips // 2) + 1
+    ring_messages = 1 + 2 * (chips // 2 - 1)
     any_spec = pl.BlockSpec(memory_space=pl.ANY)
     vmem_spec = pl.BlockSpec(memory_space=pltpu.VMEM)
     sds = jax.ShapeDtypeStruct
     dma = pltpu.SemaphoreType.DMA
-    column_map, output_full, hidden, attn_block, normed_s, query_rot, keys, values, mixed_s = (
-        pl.pallas_call(
-            partial(forward_kernel, (reps, shards, kv_start_of)),
-            out_shape=(
-                sds((d_s, block_width), BF16),
-                sds((d_s, heads_s), BF16),
-                sds((length, d_s), BF16),
-                sds((per_block, length, wide_t), F32),
-                sds((length, d_s), BF16),
-                sds((length, heads_s), BF16),
-                sds((length, kv_width), BF16),
-                sds((length, kv_width), BF16),
-                sds((length, heads_s), BF16),
-            ),
-            in_specs=[any_spec] * 2 + [vmem_spec] * 4 + [any_spec] * 9,
-            out_specs=(any_spec,) * 5 + (vmem_spec,) * 4,
-            scratch_shapes=[
-                pltpu.VMEM((d_s, heads_s), BF16),
-                pltpu.VMEM((d_s, kv_width), BF16),
-                pltpu.VMEM((d_s, kv_width), BF16),
-                pltpu.VMEM((d_s, heads_s), BF16),
-                pltpu.VMEM((d_t, heads_t), BF16),
-                pltpu.VMEM((d_t, kv_t), BF16),
-                pltpu.VMEM((d_t, kv_t), BF16),
-                pltpu.VMEM((d_t, heads_t), BF16),
-                pltpu.VMEM((length, d_s), BF16),
-                pltpu.VMEM((length, d_t), BF16),
-                pltpu.VMEM((length, d_s), BF16),
-                pltpu.VMEM((count_s, length, wide_s), BF16),
-                pltpu.VMEM((count_s, length, wide_s), BF16),
-                pltpu.VMEM((count_s, length, wide_s), BF16),
-                pltpu.VMEM((length, heads_t), BF16),
-                pltpu.VMEM((length, kv_t), BF16),
-                pltpu.VMEM((length, kv_t), BF16),
-                pltpu.VMEM((length, heads_t), BF16),
-                pltpu.VMEM((per_block, length, wide_t), F32),
-                pltpu.VMEM((most, length, wide_t), BF16),
-                pltpu.VMEM((most, length, wide_t), BF16),
-                dma((9, messages)),
-                dma((9, messages)),
-                dma((9,)),
-                dma((2, count_s)),
-                dma((2, count_s)),
-                dma((2, most)),
-                dma((2, most)),
-                dma((7,)),
-            ],
-            compiler_params=pltpu.CompilerParams(
-                collective_id=0, has_side_effects=True, vmem_limit_bytes=VMEM_BYTES
-            ),
-        )(
-            student_states,
-            teacher_states,
-            student_gain.reshape(1, -1),
-            teacher_gain.reshape(1, -1),
-            cosine,
-            sine,
-            student_query,
-            student_key,
-            student_value,
-            student_output,
-            teacher_query,
-            teacher_key,
-            teacher_value,
-            teacher_output,
-            projection,
-        )
-    )
-    attn_block = jnp.transpose(attn_block, (1, 0, 2)).reshape(length, block_width)
-    own_states = lax.dynamic_slice_in_dim(teacher_states, shard_index * block_width, block_width, 1)
-    teacher_hidden = own_states.astype(F32) + attn_block
-    scaling = 1.0 / math.sqrt(reps * length)
-    predicted = jnp.dot(hidden, column_map, preferred_element_type=F32)
-    grad_pred = ((predicted - teacher_hidden) * scaling).astype(BF16)
-    grad_hidden = pl.pallas_call(
-        partial(gradient_kernel, (reps, shards)),
-        out_shape=sds((length, d_s), BF16),
-        in_specs=[vmem_spec, any_spec],
-        out_specs=vmem_spec,
+
+    def vmem(*shape, dtype=BF16):
+        return pltpu.VMEM(shape, dtype)
+
+    _, query_grad, output_grad = pl.pallas_call(
+        partial(step_kernel, (reps, shards, kv_start_of)),
+        out_shape=(
+            sds((d_s, block_width), BF16),
+            sds((rows, heads_s), F32),
+            sds((rows, heads_s), F32),
+        ),
+        in_specs=[any_spec] * 2 + [vmem_spec] * 4 + [any_spec] * 9,
+        out_specs=(any_spec, vmem_spec, vmem_spec),
         scratch_shapes=[
-            pltpu.VMEM((d_s, block_width), BF16),
-            pltpu.VMEM((count_s, length, wide_s), BF16),
-            pltpu.VMEM((count_s, length, wide_s), BF16),
-            pltpu.VMEM((count_s, length, wide_s), BF16),
+            vmem(d_s, heads_s),
+            vmem(d_s, kv_width),
+            vmem(d_s, kv_width),
+            vmem(d_s, heads_s),
+            vmem(d_t, heads_t),
+            vmem(d_t, kv_t),
+            vmem(d_t, kv_t),
+            vmem(d_t, heads_t),
+            vmem(length, d_s),
+            vmem(length, d_t),
+            vmem(length, d_s),
+            vmem(count_s, length, wide_s),
+            vmem(count_s, length, wide_s),
+            vmem(count_s, length, wide_s),
+            vmem(length, heads_s),
+            vmem(length, kv_width),
+            vmem(length, kv_width),
+            vmem(length, heads_s),
+            vmem(length, heads_t),
+            vmem(length, kv_t),
+            vmem(length, kv_t),
+            vmem(length, heads_t),
+            vmem(per_block, length, wide_t, dtype=F32),
+            vmem(most, length, wide_t),
+            vmem(most, length, wide_t),
+            vmem(length, heads_s, dtype=F32),
+            vmem(2, ring_messages, rows // 2, heads_s),
+            vmem(2, ring_messages, rows // 2, heads_s),
+            dma((9, messages)),
+            dma((9, messages)),
+            dma((9,)),
             dma((2, count_s)),
             dma((2, count_s)),
-            dma((1,)),
+            dma((2, count_s)),
+            dma((2, count_s)),
+            dma((2, most)),
+            dma((2, most)),
+            dma((2, chips)),
+            dma((2, chips)),
+            dma((2, 2, ring_messages)),
+            dma((2, 2, ring_messages)),
+            dma((4,)),
+            dma((2 + length // wide_s,)),
         ],
         compiler_params=pltpu.CompilerParams(
-            collective_id=1, has_side_effects=True, vmem_limit_bytes=VMEM_BYTES
+            collective_id=0, has_side_effects=True, vmem_limit_bytes=VMEM_BYTES
         ),
-    )(grad_pred, column_map)
-    grad_mixed = jnp.dot(grad_hidden, output_full, preferred_element_type=F32)
-    _, pullback = jax.vjp(
-        partial(attend, keys=keys, values=values, head_dim=HD), query_rot.astype(F32)
+    )(
+        student_states,
+        teacher_states,
+        student_gain.reshape(1, -1),
+        teacher_gain.reshape(1, -1),
+        jnp.asarray(cosine),
+        jnp.asarray(sine),
+        student_query,
+        student_key,
+        student_value,
+        student_output,
+        teacher_query,
+        teacher_key,
+        teacher_value,
+        teacher_output,
+        projection,
     )
-    grad_rot = pullback(grad_mixed)[0]
-    grad_query = rotate(grad_rot, cosine, -sine).astype(BF16)
-    out_term = jnp.dot(grad_hidden.T, mixed_s, preferred_element_type=F32)
-    query_term = jnp.dot(normed_s.T, grad_query, preferred_element_type=F32)
-    return (halving_scatter(query_term, "rep"), halving_scatter(out_term, "rep"))
+    return (query_grad, output_grad)
 
 
 def solution(mesh):

time: 371 us -> 320 us (0.86)
  Pallas kernels: 285 us -> 314 us
  waiting for transfers between devices: 22.8 us -> 0 us
  matrix products: 22.1 us -> 0 us
  local copies, waits for them, and re-layouts: 20.2 us -> 5.65 us
  other arithmetic: 10.3 us -> 0 us
  starting transfers between devices: 8.82 us -> 0 us
    pallas_call x2 -> x1, Pallas kernels: 285 us -> 314 us  [local(): pl.pallas_call(partial(step_kernel, (reps, shards, kv_start_of)), out_sha...]
    ppermute x12 -> x0, waiting for transfers between devices: 22.8 us -> none  [halving_scatter(): lax.ppermute(sent.astype(BF16), axis, [(i, i ^ 1 << bit) for i in range(c...]
    dot_general x6 -> x0, matrix products: 17.9 us -> none  [the longest x1 9.91 us: local(): predicted = jnp.dot(hidden, column_map, preferred_element_type=F32)]
    ppermute x12 -> x0, starting transfers between devices: 8.82 us -> none  [halving_scatter(): lax.ppermute(sent.astype(BF16), axis, [(i, i ^ 1 << bit) for i in range(c...]
    convert_element_type x12 -> x0, local copies, waits for them, and re-layouts: 6.64 us -> none  [halving_scatter(): sent.astype(BF16)]
    add x12 -> x0, other arithmetic: 4.89 us -> none  [halving_scatter(): part = kept.astype(F32) + came.astype(F32)]
    reshape x1 -> x0, matrix products: 4.17 us -> none  [attend(): return mixed.reshape(length, -1)]
    slice x3 -> x0, local copies, waits for them, and re-layouts: 4.16 us -> none  [the longest x2 4.11 us: halving_scatter(): term[:, half * width:(half + 1) * width]]
  transfers between devices with their start and end apart: 12 -> 0, of which waited for: 6 -> 0; matrix products, arithmetic and copies ran while one was open for 3% -> 0% of each run, Pallas kernels for 0% -> 0%
where the time goes in v1:
time: 320 us
  Pallas kernels  314 us (98%)
  local copies, waits for them, and re-layouts  5.65 us (2%)
    pallas_call x1, Pallas kernels, local(): pl.pallas_call(partial(step_kernel, (reps, shards, kv_start_of)), out_sha...  314 us

profile of v1, /device:TPU:0, one launch (start us, length us, event | category | flops | bytes accessed | tf_op | source)
XLA Modules:
  0.0 320.0 jit_solution(7832664304231675004)
XLA Ops:
  0.6 1.3 reshape.10.gain_s
  2.0 313.7 %shard_map.158 = (bf16[3584,1280]{1,0:T(8,128)(2,1)}, f32[448,512]{1,0:T(8,128)}, f32[448,512]{1,0:T(8,128)}) custom-call(bf16[384,3584]{1,0:T(8,128)(2,1)} %states_s.1, bf16[384,5120]{1,0:T(8,128)(2,1)} %states_t.1, f32[1,3584]{1,0:T(1,128)} %reshape.10.gain_s, f32[1,5120]{1,0:T(1,128)} %bitcast.1, f32[384,128]{1,0:T(8,128)} %constant.4.clone.cosine, ...), custom_call_target="tpu_custom_call" | custom-call | tf_op jit(solution)/shard_map/pallas_call | solution.py:865
  315.7 2.2 copy.19
  317.9 2.2 copy.20

commit v2 on v1

--- a/solution.py
+++ b/solution.py
@@ -20,6 +20,7 @@
 BF16 = jnp.bfloat16
 VMEM_BYTES = 67_000_000
 LAG = 2
+AT = {"P1": 4, "P2a": 8, "P2b": 18, "P2a far": 21, "P2b far": 26, "P3": 32, "P4": 10, "P4 far": 13}
 
 
 def tables(length):
@@ -148,12 +149,13 @@
                 self.copy(base + step, target, owner, self.part_of(step + 1, way)).start()
             self.copy(2 * h + base + step, p.partner, owner, self.part_of(step, way)).start()
 
-    def finish(self):
+    def finish(self, first, last):
         p = self.place
         h = self.half
-        self.local().wait()
-        self.copy(2 * h, p.partner, p.partner, None).wait_recv()
-        for step in range(1, h + 1):
+        if first == 1:
+            self.local().wait()
+            self.copy(2 * h, p.partner, p.partner, None).wait_recv()
+        for step in range(first, last + 1):
             for way, sign in ((0, -1), (1, 1)):
                 owner = p.rep_at(sign * step, 1 - p.core)
                 self.copy(
@@ -264,10 +266,17 @@
     return lambda: lax.fori_loop(0, count, drain, 0)
 
 
-def line_scatter(place, per_block, produce, own, rightward, leftward, send_sem, recv_sem, hooks):
+def turn_of(u, late):
+    return jnp.where((late == 0) & (u < 2), 1 - u, u)
+
+
+def line_scatter(
+    place, per_block, produce, own, late, rightward, leftward, send_sem, recv_sem, hooks
+):
     z = place.z
     ends = place.shards - 1
-    waves = ends * per_block + LAG * ends
+    count = ends * per_block
+    waves = count + LAG * ends
 
     def copy(way, q):
         buffer = (rightward, leftward)[way]
@@ -279,24 +288,23 @@
             device_id={"shard": (z + 1, z - 1)[way]},
         )
 
-    def first_own(t, carry):
-        own[t] = produce(z * per_block + t).astype(BF16).astype(F32)
-        return carry
-
-    lax.fori_loop(0, per_block, first_own, 0)
+    def block_at(way, q):
+        last = late if way else ends - late
+        return turn_of(lax.div(q, per_block), last)
 
     def wave_body(w, carry):
         for way in range(2):
             line = (z, ends - z)[way]
             q = w - LAG * line
-            past = (ends - line) * per_block
+            valid = (q >= 0) & (q < count)
+            place_q = jnp.clip(q, 0, count - 1)
+            block = block_at(way, place_q)
+            chunk = lax.rem(place_q, per_block)
             buffer = (rightward, leftward)[way]
             before = line > 0
 
-            @pl.when((q >= 0) & (q < past))
+            @pl.when(valid & (block < ends - line))
             def _():
-                block = lax.div(q, per_block)
-                chunk = lax.rem(q, per_block)
                 target = (ends - block, block)[way]
                 term = produce(target * per_block + chunk).astype(BF16)
 
@@ -311,10 +319,10 @@
 
                 copy(way, q).start()
 
-            @pl.when(before & (q >= past) & (q < past + per_block))
+            @pl.when(valid & before & (block == ends - line))
             def _():
                 copy(way, q).wait_recv()
-                own[q - past] += buffer[q].astype(F32)
+                own[chunk] += buffer[q].astype(F32)
 
         run_hooks(hooks, w, waves)
         return carry
@@ -327,10 +335,13 @@
             line = (z, ends - z)[way]
 
             def drain(q, carry):
-                copy(way, q).wait_send()
+                @pl.when(block_at(way, q) < ends - line)
+                def _():
+                    copy(way, q).wait_send()
+
                 return carry
 
-            lax.fori_loop(0, (ends - line) * per_block, drain, 0)
+            lax.fori_loop(0, count, drain, 0)
 
     return finish
 
@@ -435,7 +446,7 @@
         at = pl.ds(pl.multiple_of(i * block, block), block)
         rows = states[at, :].astype(F32)
         meansq = jnp.sum(rows * rows, axis=-1, keepdims=True) * (1.0 / width)
-        states[at, :] = (rows * lax.rsqrt(meansq + norm_epsilon) * gain[...]).astype(BF16)
+        states[at, :] = (rows * lax.rsqrt(meansq + norm_epsilon) * gain[...][None, :]).astype(BF16)
         return carry
 
     lax.fori_loop(0, length // block, body, 0)
@@ -590,11 +601,20 @@
         for weight in groups[name]:
             weight.relay(step)
 
-    def finish(name):
-        for step in range(2, half + 1):
+    def near(name):
+        for step in range(2, half):
             relay(name, step)
         for weight in groups[name]:
-            weight.finish()
+            weight.finish(1, half - 1)
+
+    def far(name):
+        relay(name, half)
+        for weight in groups[name]:
+            weight.finish(half, half)
+
+    def finish(name):
+        near(name)
+        far(name)
 
     def drain(names):
         for name in names:
@@ -627,7 +647,7 @@
     heads = sq.shape[1] // HD
     group = heads // (kv_width // HD)
     attention(query_s, key_s, value_s, mixed_s, 0, heads, group)
-    finish("P1")
+    near("P1")
     in_h.wait()
 
     count, _, width = own_s.shape
@@ -637,45 +657,61 @@
         states_t.at[:, states_at], normed_t.at[:, 0:block_width], copies.at[3]
     )
 
+    steps = ring_order(place.chips)
+    per_chip = count // place.chips
+    in_order = per_chip * place.chips == count
+    if not in_order:
+        far("P1")
+
+    def tile_at(j, order):
+        if not in_order:
+            return j
+        turn = lax.div(j, per_chip)
+        chip = 0
+        for i, step in enumerate(order):
+            chip = chip + jnp.where(turn == i, lax.div(place.rep_at(step, 0), 2), 0)
+        return chip * per_chip + lax.rem(j, per_chip)
+
     def produce_s(j):
-        return dot_nt(mixed_s[...], so[span(j, width), :])
+        return dot_nt(mixed_s[...], so[span(tile_at(j, steps[::-1]), width), :])
 
     def consume_s(j, total):
-        at = span(j, width)
+        at = span(tile_at(j, steps[::-1]), width)
         hidden[:, at] = (hidden[:, at].astype(F32) + total).astype(BF16)
 
     t_tile = tile_of(tq.shape[1])
     t_kv = tile_of(tk.shape[1])
     t_heads = tq.shape[1] // HD
     t_group = t_heads // (tk.shape[1] // HD)
-    hooks = [
-        (5, lambda: relay("P2a", 1)),
-        (14, lambda: relay("P2b", 1)),
-        (14, lambda: start("P3")),
-        (17, lambda: finish("P2a")),
-        (22, lambda: finish("P2b")),
+    hooks = [(AT["P1"], lambda: far("P1"))] if in_order else []
+    hooks += [
+        (AT["P2a"], lambda: relay("P2a", 1)),
+        (AT["P2b"], lambda: relay("P2b", 1)),
+        (AT["P2b"], lambda: start("P3")),
+        (AT["P2a far"], lambda: finish("P2a")),
+        (AT["P2b far"], lambda: finish("P2b")),
     ]
-    wave = 22
+    tasks = []
     for t in range(tk.shape[1] // t_kv):
-        hooks.append((wave, partial(project, normed_t, tk, key_t, cosine, sine, t, 1, t_kv)))
-        wave += 1
-        hooks.append((wave, partial(project, normed_t, tv, value_t, None, None, t, 1, t_kv)))
-        wave += 1
+        tasks.append(partial(project, normed_t, tk, key_t, cosine, sine, t, 1, t_kv))
+        tasks.append(partial(project, normed_t, tv, value_t, None, None, t, 1, t_kv))
     for t in range(tq.shape[1] // t_tile):
-        hooks.append((wave, partial(project, normed_t, tq, query_t, cosine, sine, t, 1, t_tile)))
-        wave += 1
-    hooks.append((wave, lambda: drain(("P0", "P1", "P2a", "P2b"))))
-    hooks.append((wave, in_b.start))
+        tasks.append(partial(project, normed_t, tq, query_t, cosine, sine, t, 1, t_tile))
+    tasks.append(lambda: drain(("P0", "P1", "P2a", "P2b")))
+    tasks.append(in_b.start)
     for h in range(t_heads):
-        hooks.append((wave, partial(attention, query_t, key_t, value_t, mixed_t, h, 1, t_group)))
-        wave += 1
-    hooks.append((wave - 2, lambda: relay("P3", 1)))
-    hooks.append((wave - 2, lambda: start("P4")))
+        tasks.append(partial(attention, query_t, key_t, value_t, mixed_t, h, 1, t_group))
+    hooks += [(AT["P2b far"] + i // 2, task) for i, task in enumerate(tasks)]
+    hooks.append((AT["P3"], lambda: relay("P3", 1)))
+    hooks.append((AT["P3"], lambda: start("P4")))
     drain_s = line_sum(
         place, count, produce_s, consume_s, own_s, right_s, left_s, sum_send, sum_recv, hooks
     )
     drain_s()
-    finish("P3")
+    near("P3")
+    by_chip = shards == place.chips
+    if not by_chip:
+        far("P3")
 
     per_block, _, width_t = attn_t.shape
     in_b.wait()
@@ -706,10 +742,19 @@
         if t + 2 < per_block:
             column_copy(t + 2).start()
 
-    hooks = [(2, lambda: relay("P4", 1)), (8, lambda: finish("P4")), (8, first_columns)]
-    hooks += [(9 + t, partial(predict, t)) for t in range(per_block)]
+    def own_terms():
+        for t in range(per_block):
+            attn_t[t] += produce_t(place.z * per_block + t).astype(BF16).astype(F32)
+
+    attn_t[...] = jnp.zeros_like(attn_t)
+    hooks = [(per_block - 1, lambda: far("P3"))] if by_chip else []
+    hooks += [(per_block, own_terms), (AT["P4"], lambda: relay("P4", 1))]
+    hooks += [(AT["P4 far"], lambda: finish("P4")), (AT["P4 far"], first_columns)]
+    hooks += [(AT["P4 far"] + 1 + t, partial(predict, t)) for t in range(per_block)]
+    opposite = lax.div(place.rep_at(half, 0), 2)
     drain_t = line_scatter(
-        place, per_block, produce_t, attn_t, right_t, left_t, scatter_send, scatter_recv, hooks
+        place, per_block, produce_t, attn_t, opposite if by_chip else place.shards - 1, right_t,
+        left_t, scatter_send, scatter_recv, hooks,
     )
     scaling = 1.0 / math.sqrt(reps * length)
     grad_pred = normed_t.at[:, 0:block_width]
@@ -730,25 +775,12 @@
     query_sum = RingScatter(
         place, so, slot(place.chips), ring_query, query_grad, 1, pair_sems, ring_sems
     )
-    steps = ring_order(place.chips)
-    per_chip = count // place.chips
-    in_order = per_chip * place.chips == count
-
-    def tile_at(j):
-        if not in_order:
-            return j
-        turn = lax.div(j, per_chip)
-        chip = 0
-        for i, step in enumerate(steps):
-            chip = chip + jnp.where(turn == i, lax.div(place.rep_at(step, 0), 2), 0)
-        return chip * per_chip + lax.rem(j, per_chip)
-
     slots = length // width
 
     def rows_copy(j):
         slot_at = lax.rem(j, slots)
         return pltpu.make_async_copy(
-            map_full.at[span(tile_at(j), width)],
+            map_full.at[span(tile_at(j, steps), width)],
             normed_t.at[span(slot_at, width), block_width : 2 * block_width],
             map_sems.at[2 + slot_at],
         )
@@ -767,7 +799,7 @@
     grad_mixed[...] = jnp.zeros_like(grad_mixed)
 
     def consume_b(j, total):
-        at = span(tile_at(j), width)
+        at = span(tile_at(j, steps), width)
         grad = total.astype(BF16)
         grad_mixed[...] += jnp.dot(grad, so[at, :], preferred_element_type=F32)
         sq[at, :] = dot_tn(grad, mixed_s[...]).astype(BF16)
@@ -922,8 +954,8 @@
     )(
         student_states,
         teacher_states,
-        student_gain.reshape(1, -1),
-        teacher_gain.reshape(1, -1),
+        student_gain,
+        teacher_gain,
         jnp.asarray(cosine),
         jnp.asarray(sine),
         student_query,

time: 320 us -> 299 us (0.934)
  Pallas kernels: 314 us -> 294 us
    pallas_call x1, Pallas kernels: 314 us -> 294 us  [local(): pl.pallas_call(partial(step_kernel, (reps, shards, kv_start_of)), out_sha...]
where the time goes in v2:
time: 299 us
  Pallas kernels  294 us (98%)
  local copies, waits for them, and re-layouts  4.32 us (1%)
    pallas_call x1, Pallas kernels, local(): pl.pallas_call(partial(step_kernel, (reps, shards, kv_start_of)), out_sha...  294 us

profile of v2, /device:TPU:0, one launch (start us, length us, event | category | flops | bytes accessed | tf_op | source)
XLA Modules:
  0.0 298.8 jit_solution(16880237585795799255)
XLA Ops:
  0.6 293.8 %shard_map.158 = (bf16[3584,1280]{1,0:T(8,128)(2,1)}, f32[448,512]{1,0:T(8,128)}, f32[448,512]{1,0:T(8,128)}) custom-call(bf16[384,3584]{1,0:T(8,128)(2,1)} %states_s.1, bf16[384,5120]{1,0:T(8,128)(2,1)} %states_t.1, f32[3584]{0:T(1024)} %gain_s.1, f32[5120]{0:T(1024)} %gain_t.1, f32[384,128]{1,0:T(8,128)} %constant.4.clone.cosine, ...), custom_call_target="tpu_custom_call" | custom-call | tf_op jit(solution)/shard_map/pallas_call | solution.py:897
  294.5 2.2 copy.19
  296.6 2.2 copy.20

commit v3 on v2

--- a/solution.py
+++ b/solution.py
@@ -20,7 +20,7 @@
 BF16 = jnp.bfloat16
 VMEM_BYTES = 67_000_000
 LAG = 2
-AT = {"P1": 4, "P2a": 8, "P2b": 18, "P2a far": 21, "P2b far": 26, "P3": 32, "P4": 10, "P4 far": 13}
+AT = {"P1": 10, "P2a": 8, "P2b": 18, "P2b near": 20, "P2a far": 24, "P2b far": 26, "P3": 40, "P4": 9, "P4 far": 14}
 
 
 def tables(length):
@@ -383,7 +383,7 @@
         m = self.message(step, part)
         return pltpu.make_async_remote_copy(
             src_ref=self.half_of(self.pair(i), part),
-            dst_ref=self.ring.at[way, m],
+            dst_ref=self.ring(way, m),
             send_sem=self.ring_sems[0].at[self.index, way, m],
             recv_sem=self.ring_sems[1].at[self.index, way, m],
             device_id={"rep": (self.place.right, self.place.left)[way]},
@@ -404,17 +404,25 @@
 
     def incoming(self, way, step, part, i):
         self.ring_copy(way, step, part, i).wait_recv()
-        return self.ring[way, self.message(step, part)].astype(F32)
-
-    def forward(self, i):
-        self.pair_copy(i).wait_recv()
-        if self.steps[i] != 0:
-            for way, step, part, has in self.moves(i):
+        return self.ring(way, self.message(step, part))[...].astype(F32)
+
+    def send(self, i, summed):
+        for way, step, part, has in self.moves(i):
+            if has == summed:
                 value = self.fresh(i, part)
                 if has:
                     value = value + self.incoming(way, step + 1, part, i)
                 self.half_of(self.pair(i), part)[...] = value.astype(BF16)
                 self.ring_copy(way, step, part, i).start()
+
+    def send_fresh(self, i):
+        self.pair_copy(i).wait_recv()
+        if self.steps[i] != 0:
+            self.send(i, False)
+
+    def send_sums(self, i):
+        if self.steps[i] != 0:
+            self.send(i, True)
             return
         for part in range(2):
             value = self.fresh(i, part)
@@ -422,6 +430,10 @@
                 if part == way or self.half > 1:
                     value = value + self.incoming(way, 1, part, i)
             self.half_of(self.out, part)[...] = value
+
+    def forward(self, i):
+        self.send_fresh(i)
+        self.send_sums(i)
 
     def drain(self):
         for i, e in enumerate(self.steps):
@@ -470,6 +482,30 @@
         return carry
 
     lax.fori_loop(first, first + count, body, 0)
+
+
+def project_near(place, normed, weight, total, t, tile):
+    at = span(t, tile)
+    size = weight.shape[0] // place.chips
+    value = None
+    for step in ring_order(place.chips)[1:]:
+        rows = span(lax.div(place.rep_at(step, 0), 2), size)
+        term = jnp.dot(normed[:, rows], weight[rows, at], preferred_element_type=F32)
+        value = term if value is None else value + term
+    total[...] = value
+
+
+def project_far(place, normed, weight, total, out, cosine, sine, t, tile):
+    at = span(t, tile)
+    size = weight.shape[0] // place.chips
+    rows = span(lax.div(place.rep_at(place.chips // 2, 0), 2), size)
+    value = total[...] + jnp.dot(normed[:, rows], weight[rows, at], preferred_element_type=F32)
+    if cosine is None:
+        out[:, at] = value.astype(BF16)
+    else:
+        for head in range(tile // HD):
+            part = turned(value[:, head * HD : (head + 1) * HD], cosine[...], sine[...])
+            out[:, t * tile + head * HD : t * tile + (head + 1) * HD] = part.astype(BF16)
 
 
 def soft(scores):
@@ -556,13 +592,13 @@
     grad_mixed,
     ring_out,
     ring_query,
+    query_total,
+    out_total,
     gather_send,
     gather_recv,
     gather_local,
     sum_send,
     sum_recv,
-    back_send,
-    back_recv,
     scatter_send,
     scatter_recv,
     pair_send,
@@ -688,15 +724,34 @@
         (AT["P2a"], lambda: relay("P2a", 1)),
         (AT["P2b"], lambda: relay("P2b", 1)),
         (AT["P2b"], lambda: start("P3")),
-        (AT["P2a far"], lambda: finish("P2a")),
-        (AT["P2b far"], lambda: finish("P2b")),
+        (AT["P2b near"], lambda: near("P2a")),
+        (AT["P2b near"], lambda: near("P2b")),
+        (AT["P2a far"], lambda: far("P2a")),
+        (AT["P2b far"], lambda: far("P2b")),
     ]
+    jobs = []
+    for t in range(tk.shape[1] // t_kv):
+        jobs.append((tk, key_t, cosine, sine, t, t_kv))
+        jobs.append((tv, value_t, None, None, t, t_kv))
+    for t in range(tq.shape[1] // t_tile):
+        jobs.append((tq, query_t, cosine, sine, t, t_tile))
     tasks = []
-    for t in range(tk.shape[1] // t_kv):
-        tasks.append(partial(project, normed_t, tk, key_t, cosine, sine, t, 1, t_kv))
-        tasks.append(partial(project, normed_t, tv, value_t, None, None, t, 1, t_kv))
-    for t in range(tq.shape[1] // t_tile):
-        tasks.append(partial(project, normed_t, tq, query_t, cosine, sine, t, 1, t_tile))
+    split = len(jobs) <= attn_t.shape[0] and t_kv == t_tile == attn_t.shape[2]
+    for i, (weight, out, cos, sin, t, wide_at) in enumerate(jobs):
+        if split:
+            hooks.append(
+                (
+                    AT["P2b near"] + i,
+                    partial(project_near, place, normed_t, weight, attn_t.at[i], t, wide_at),
+                )
+            )
+            tasks.append(
+                partial(
+                    project_far, place, normed_t, weight, attn_t.at[i], out, cos, sin, t, wide_at
+                )
+            )
+        else:
+            tasks.append(partial(project, normed_t, weight, out, cos, sin, t, 1, wide_at))
     tasks.append(lambda: drain(("P0", "P1", "P2a", "P2b")))
     tasks.append(in_b.start)
     for h in range(t_heads):
@@ -766,15 +821,30 @@
     pair_sems = (pair_send, pair_recv)
     ring_sems = (ring_send, ring_recv)
 
-    def slot(first):
-        return lambda i: tq.at[(first + i) * rows : (first + i + 1) * rows, 0:wide]
-
-    out_sum = RingScatter(
-        place, sq, slot(0), ring_out, output_grad, 0, pair_sems, ring_sems
-    )
-    query_sum = RingScatter(
-        place, so, slot(place.chips), ring_query, query_grad, 1, pair_sems, ring_sems
-    )
+    def ring_sum(index, sums, first, ring, out, columns):
+        def pair(i):
+            return tq.at[(first + i) * rows : (first + i + 1) * rows, columns]
+
+        def landing(way, m):
+            return ring.at[way, m, :, columns]
+
+        return RingScatter(
+            place, sums.at[:, columns], pair, landing, out.at[:, columns], index, pair_sems, ring_sems
+        )
+
+    parts = 2 if heads % 2 == 0 else 1
+    part_wide = wide // parts
+    cuts = [slice(c * part_wide, (c + 1) * part_wide) for c in range(parts)]
+    out_sum = ring_sum(0, sq, 0, ring_out, out_total, slice(0, wide))
+    query_sums = [
+        ring_sum(1 + c, so, place.chips, ring_query, query_total, cut) for c, cut in enumerate(cuts)
+    ]
+    out_copy = pltpu.make_async_copy(out_total, output_grad, copies.at[4])
+    query_copies = [
+        pltpu.make_async_copy(query_total.at[:, cut], query_grad.at[:, cut], copies.at[5 + c])
+        for c, cut in enumerate(cuts)
+    ]
+
     slots = length // width
 
     def rows_copy(j):
@@ -796,13 +866,17 @@
 
         return product
 
+    drain(("P3", "P4"))
     grad_mixed[...] = jnp.zeros_like(grad_mixed)
+    flips = length <= to.shape[1]
 
     def consume_b(j, total):
         at = span(tile_at(j, steps), width)
         grad = total.astype(BF16)
         grad_mixed[...] += jnp.dot(grad, so[at, :], preferred_element_type=F32)
         sq[at, :] = dot_tn(grad, mixed_s[...]).astype(BF16)
+        if flips:
+            to[at, 0:length] = normed_s[:, at].T
 
     for j in range(min(slots, count)):
         rows_copy(j).start()
@@ -810,9 +884,10 @@
     for i in range(place.chips):
         ready = (i + 1) * per_chip - 1 if in_order else count
         done.append((ready, partial(out_sum.exchange, i)))
-        done.append((ready + 3 if in_order else count, partial(out_sum.forward, i)))
+        if i < place.chips - 1:
+            done.append((ready + 3 if in_order else count, partial(out_sum.forward, i)))
     drain_b = line_sum(
-        place, count, produce_b, consume_b, own_s, right_s, left_s, back_send, back_recv, [], done
+        place, count, produce_b, consume_b, own_s, right_s, left_s, sum_send, sum_recv, [], done
     )
     grad_query = query_t.at[:, 0:wide]
 
@@ -820,31 +895,48 @@
         backward_head(h, query_s, key_s, value_s, grad_mixed, grad_query, cosine, sine, group)
         return carry
 
-    lax.fori_loop(0, heads, one_head, 0)
-
-    def query_tile(t, carry):
-        so[span(t, width), :] = dot_tn(normed_s[:, span(t, width)], grad_query[...]).astype(BF16)
-        return carry
-
-    if in_order:
+    pending = [lambda: out_sum.forward(place.chips - 1), out_copy.start]
+    for c, cut in enumerate(cuts):
+        part_heads = heads // parts
+        lax.fori_loop(c * part_heads, (c + 1) * part_heads, one_head, 0)
+        total = query_sums[c]
+
+        def query_rows(at):
+            if flips:
+                term = jnp.dot(to[at, 0:length], grad_query[:, cut], preferred_element_type=F32)
+            else:
+                term = dot_tn(normed_s[:, at], grad_query[:, cut])
+            so[at, cut] = term.astype(BF16)
+
+        def query_tile(t, carry):
+            query_rows(span(t, width))
+            return carry
+
+        if not in_order:
+            lax.fori_loop(0, count, query_tile, 0)
         for i, step in enumerate(steps):
-            first = lax.div(place.rep_at(step, 0), 2) * per_chip
-            lax.fori_loop(first, first + per_chip, query_tile, 0)
-            query_sum.exchange(i)
+            if in_order:
+                query_rows(span(lax.div(place.rep_at(step, 0), 2), per_chip * width))
+            total.exchange(i)
             if i > 0:
-                query_sum.forward(i - 1)
-        query_sum.forward(len(steps) - 1)
-    else:
-        lax.fori_loop(0, count, query_tile, 0)
-        for i in range(len(steps)):
-            query_sum.exchange(i)
-        for i in range(len(steps)):
-            query_sum.forward(i)
+                total.send_fresh(i - 1)
+            if pending and i > 0:
+                pending.pop(0)()
+        total.send_fresh(len(steps) - 1)
+        while pending:
+            pending.pop(0)()
+        pending = [partial(total.send_sums, i) for i in range(1, len(steps))]
+        pending.append(query_copies[c].start)
+    while pending:
+        pending.pop(0)()
     drain_t()
     drain_b()
-    drain(("P3", "P4"))
     out_sum.drain()
-    query_sum.drain()
+    for total in query_sums:
+        total.drain()
+    out_copy.wait()
+    for copy in query_copies:
+        copy.wait()
 
 
 def local(
@@ -902,7 +994,7 @@
             sds((rows, heads_s), F32),
         ),
         in_specs=[any_spec] * 2 + [vmem_spec] * 4 + [any_spec] * 9,
-        out_specs=(any_spec, vmem_spec, vmem_spec),
+        out_specs=(any_spec,) * 3,
         scratch_shapes=[
             vmem(d_s, heads_s),
             vmem(d_s, kv_width),
@@ -932,20 +1024,20 @@
             vmem(length, heads_s, dtype=F32),
             vmem(2, ring_messages, rows // 2, heads_s),
             vmem(2, ring_messages, rows // 2, heads_s),
+            vmem(rows, heads_s, dtype=F32),
+            vmem(rows, heads_s, dtype=F32),
             dma((9, messages)),
             dma((9, messages)),
             dma((9,)),
             dma((2, count_s)),
             dma((2, count_s)),
-            dma((2, count_s)),
-            dma((2, count_s)),
             dma((2, most)),
             dma((2, most)),
-            dma((2, chips)),
-            dma((2, chips)),
-            dma((2, 2, ring_messages)),
-            dma((2, 2, ring_messages)),
-            dma((4,)),
+            dma((3, chips)),
+            dma((3, chips)),
+            dma((3, 2, ring_messages)),
+            dma((3, 2, ring_messages)),
+            dma((7,)),
             dma((2 + length // wide_s,)),
         ],
         compiler_params=pltpu.CompilerParams(

time: 299 us -> 291 us (0.973)
  Pallas kernels: 294 us -> 286 us
    pallas_call x1, Pallas kernels: 294 us -> 286 us  [local(): pl.pallas_call(partial(step_kernel, (reps, shards, kv_start_of)), out_sha...]
where the time goes in v3:
time: 291 us
  Pallas kernels  286 us (98%)
  local copies, waits for them, and re-layouts  4.32 us (1%)
    pallas_call x1, Pallas kernels, local(): pl.pallas_call(partial(step_kernel, (reps, shards, kv_start_of)), out_sha...  286 us

profile of v3, /device:TPU:0, one launch (start us, length us, event | category | flops | bytes accessed | tf_op | source)
XLA Modules:
  0.0 290.7 jit_solution(8397790594130105606)
XLA Ops:
  0.6 285.8 %shard_map.158 = (bf16[3584,1280]{1,0:T(8,128)(2,1)}, f32[448,512]{1,0:T(8,128)}, f32[448,512]{1,0:T(8,128)}) custom-call(bf16[384,3584]{1,0:T(8,128)(2,1)} %states_s.1, bf16[384,5120]{1,0:T(8,128)(2,1)} %states_t.1, f32[3584]{0:T(1024)} %gain_s.1, f32[5120]{0:T(1024)} %gain_t.1, f32[384,128]{1,0:T(8,128)} %constant.4.clone.cosine, ...), custom_call_target="tpu_custom_call" | custom-call | tf_op jit(solution)/shard_map/pallas_call | solution.py:989
  286.4 2.2 copy.19
  288.6 2.2 copy.20

commit v4 on v3

--- a/solution.py
+++ b/solution.py
@@ -20,7 +20,7 @@
 BF16 = jnp.bfloat16
 VMEM_BYTES = 67_000_000
 LAG = 2
-AT = {"P1": 10, "P2a": 8, "P2b": 18, "P2b near": 20, "P2a far": 24, "P2b far": 26, "P3": 40, "P4": 9, "P4 far": 14}
+AT = {"P1": 10, "P2a": 8, "P2b": 18, "P2b near": 20, "P2a far": 24, "P2b far": 26, "P3": 40, "P4": 9, "P4 far": 13}
 
 
 def tables(length):
@@ -939,6 +939,23 @@
         copy.wait()
 
 
+def place_kernel(query_from, output_from, query_to, output_to, query_held, output_held, sems):
+    moves = []
+    for i, (source, held, target) in enumerate(
+        ((query_from, query_held, query_to), (output_from, output_held, output_to))
+    ):
+        moves.append(pltpu.make_async_copy(source, held, sems.at[i]))
+        moves.append(pltpu.make_async_copy(held, target, sems.at[2 + i]))
+    moves[0].start()
+    moves[2].start()
+    moves[0].wait()
+    moves[1].start()
+    moves[2].wait()
+    moves[3].start()
+    moves[1].wait()
+    moves[3].wait()
+
+
 def local(
     reps,
     shards,
@@ -1060,7 +1077,13 @@
         teacher_output,
         projection,
     )
-    return (query_grad, output_grad)
+    return pl.pallas_call(
+        place_kernel,
+        out_shape=(sds((rows, heads_s), F32),) * 2,
+        in_specs=[any_spec] * 2,
+        out_specs=(any_spec,) * 2,
+        scratch_shapes=[vmem(rows, heads_s, dtype=F32)] * 2 + [dma((4,))],
+    )(query_grad, output_grad)
 
 
 def solution(mesh):

time: 291 us -> 288 us (0.990)
  local copies, waits for them, and re-layouts: 4.32 us -> 0 us
    unnamed x2 -> x0, local copies, waits for them, and re-layouts: 4.32 us -> none
where the time goes in v4:
time: 288 us
  Pallas kernels  287 us (100%)
    pallas_call x1, Pallas kernels, local(): pl.pallas_call(partial(step_kernel, (reps, shards, kv_start_of)), out_sha...  284 us

profile of v4, /device:TPU:0, one launch (start us, length us, event | category | flops | bytes accessed | tf_op | source)
XLA Modules:
  0.0 287.5 jit_solution(1488854998664901351)
XLA Ops:
  0.6 284.3 %shard_map.158 = (bf16[3584,1280]{1,0:T(8,128)(2,1)}, f32[448,512]{1,0:T(8,128)}, f32[448,512]{1,0:T(8,128)}) custom-call(bf16[384,3584]{1,0:T(8,128)(2,1)} %states_s.1, bf16[384,5120]{1,0:T(8,128)(2,1)} %states_t.1, f32[3584]{0:T(1024)} %gain_s.1, f32[5120]{0:T(1024)} %gain_t.1, f32[384,128]{1,0:T(8,128)} %constant.4.clone.cosine, ...), custom_call_target="tpu_custom_call" | custom-call | tf_op jit(solution)/shard_map/pallas_call | solution.py:1006
  284.9 2.4 shard_map.159
